TPU v7x, 256 devices: a whole 4x4x8 slice. The times are simulated.
256 devices in a mesh: dp: 32 (over z_hi, y, core), node: 8 (over z_lo, x).
Axes of the slice: x: 4, y: 4, z: 8 (z_hi: 4, z_lo: 2; z = z_hi * 2 + z_lo), core: 2. Of those that a mesh axis runs over, the one named last changes fastest.
Arguments:
- node_feats: bfloat16 [6144, 25, 128], P(('dp', 'node')), may hold values from -2 to 2
- cotangent: bfloat16 [6144, 25, 128], P(('dp', 'node')), may hold values from -3 to 3
- wigner: bfloat16 [13, 25, 65536], P(None, None, ('dp', 'node')), may hold values from -1.25 to 1.25
- radial: bfloat16 [2, 65536, 128], P(None, ('dp', 'node')), may hold values from 0.29882812 to 3
- edge_src: int32 [65536], P(('dp', 'node')), may hold values from 0 to 23
- edge_dst: int32 [65536], P(('dp', 'node')), may hold values from 0 to 23
- edge_count: int32 [256], P(('dp', 'node')), may hold values from 128 to 256
- params: float32 [2, 933888], P(None, ('dp', 'node')), may hold values from -0.5 to 0.5
- moment1: float32 [2, 933888], P(None, ('dp', 'node')), may hold values from -3 to 3
- moment2: float32 [2, 933888], P(None, ('dp', 'node')), may hold values from 1 to 100
Outputs:
- new_params: float32 [2, 933888], P(None, ('dp', 'node'))
- new_moment1: float32 [2, 933888], P(None, ('dp', 'node'))
- new_moment2: float32 [2, 933888], P(None, ('dp', 'node'))
Inputs may be any that keep to these rules, and one draw needn't show every extreme that they name: `edge_src`: atom numbers within the edge's own structure. `edge_dst`: atom numbers within the edge's own structure. `edge_count`: slots from this number on within a structure are padding.
All inputs are finite; a program needn't handle non-finite values.
Results may differ from a plain program's by a relative error of at most 0.017.
Values may be sent and summed in bfloat16 or wider, within the bound.
No kernel may reach another device: no remote copies, remote signals or barrier semaphores. Data moves between devices by JAX's collectives and lax.ppermute only.
A program may use at most 64 MiB of HBM per device.

v0:
```python
import functools

import jax
import jax.numpy as jnp
from jax import lax
from jax.experimental import pallas as pl
from jax.experimental.pallas import tpu as pltpu
from jax.sharding import Mesh
from jax.sharding import PartitionSpec as P

F32 = jnp.float32
BF16 = jnp.bfloat16
AVG = 10
AXES = ("zh", "y", "core", "zl", "x")
SIZES = (4, 4, 2, 2, 4)
NEAR = ("y", "zl")
FAR = ("zh", "x")
LANES = 128


def mm(a, b):
    return lax.dot_general(a, b, (((1,), (0,)), ((), ())), preferred_element_type=F32)


def mm_bt(a, b):
    return lax.dot_general(a, b, (((1,), (1,)), ((), ())), preferred_element_type=F32)


def mm_at(a, b):
    return lax.dot_general(a, b, (((0,), (0,)), ((), ())), preferred_element_type=F32)


def prep_kernel(nat, wig_ref, src_ref, dst_ref, srcc_ref, dstc_ref, x_ref, rad_ref, a_ref, b_ref, bt_ref, d_ref, dt_ref):
    rows, coef, edges = wig_ref.shape
    wide = coef * nat
    chan = x_ref.shape[1]
    lane = lax.broadcasted_iota(jnp.int32, (coef, wide), 1)
    start = lax.broadcasted_iota(jnp.int32, (coef, wide), 0) * nat
    spread = ((lane >= start) & (lane < start + nat)).astype(BF16)
    lane_e = lax.broadcasted_iota(jnp.int32, (edges, wide), 1) % nat
    row_e = lax.broadcasted_iota(jnp.int32, (wide, edges), 0) % nat
    pick_src = (lane_e == srcc_ref[...]).astype(F32).astype(BF16)
    pick_dst = (lane_e == dstc_ref[...]).astype(F32).astype(BF16)
    pick_src_t = (row_e == src_ref[...]).astype(F32).astype(BF16)
    pick_dst_t = (row_e == dst_ref[...]).astype(F32).astype(BF16)
    x = x_ref[...]
    rad = rad_ref[...].astype(F32)
    for k in range(rows):
        w = wig_ref[k]
        e_wide = mm_at(w, spread).astype(BF16)
        wide_e = mm_at(spread, w).astype(BF16)
        b = e_wide * pick_src
        b_ref[k] = b
        d_ref[k] = e_wide * pick_dst
        bt_ref[k] = wide_e * pick_src_t
        dt_ref[k] = wide_e * pick_dst_t
        a_ref[:, k * chan : (k + 1) * chan] = (mm(b, x) * rad).astype(BF16)


def rotate(b_ref, x, rad, a_ref):
    chan = x.shape[1]
    for k in range(b_ref.shape[0]):
        a_ref[:, k * chan : (k + 1) * chan] = (mm(b_ref[k], x) * rad).astype(BF16)


def mix(a_ref, w0, wr, wi, m_ref):
    kz, ko = w0.shape[0], wr.shape[0]
    m_ref[:, :kz] = mm(a_ref[:, :kz], w0[...]).astype(BF16)
    ap = a_ref[:, kz : kz + ko]
    am = a_ref[:, kz + ko :]
    m_ref[:, kz : kz + ko] = (mm(ap, wr[...]) - mm(am, wi[...])).astype(BF16)
    m_ref[:, kz + ko :] = (mm(ap, wi[...]) + mm(am, wr[...])).astype(BF16)


def back_to_nodes(t_ref, m_ref, chan):
    total = mm(t_ref[0], m_ref[:, :chan])
    for k in range(1, t_ref.shape[0]):
        total = total + mm(t_ref[k], m_ref[:, k * chan : (k + 1) * chan])
    return total


def gate(out, nat):
    o = out.reshape(-1, nat, out.shape[1])
    s = o[0]
    sig = jax.nn.sigmoid(s)
    h = jnp.concatenate([(s * sig)[None], o[1:] * sig[None]], axis=0)
    return h.reshape(out.shape)


def gate_back(dh, out, nat):
    o = out.reshape(-1, nat, out.shape[1])
    g = dh.reshape(o.shape)
    s = o[0]
    sig = jax.nn.sigmoid(s)
    slope = sig * (1.0 - sig)
    down = jnp.sum(g[1:] * o[1:], axis=0) * slope + g[0] * (sig + s * slope)
    d = jnp.concatenate([down[None], g[1:] * sig[None]], axis=0)
    return d.reshape(out.shape)


def pieces(kz, ko):
    first = kz * (kz // LANES)
    second = first + ko * (ko // LANES)
    return ((0, kz, kz // LANES), (first, ko, ko // LANES), (second, ko, ko // LANES))


def chunk_at(g, core, zh):
    y, zl = divmod(g, 2)
    return ((zh * 4 + y) * 2 + core) * 2 + zl


def unpack(core, mine, other, flat, stage, weights):
    groups, rows, _ = mine.shape
    part = rows // 4
    for g in range(groups):
        m = mine[g].astype(F32)
        o = other[g].astype(F32)
        for c in range(2):
            stage[c] = jnp.where(core == c, m, o)
            for zh in range(4):
                at = chunk_at(g, c, zh) * part
                flat[at : at + part] = stage[c, zh * part : (zh + 1) * part]
    for ref, (first, side, step) in zip(weights, pieces(weights[0].shape[0], weights[1].shape[0])):
        for q in range(step):
            ref[:, q * LANES : (q + 1) * LANES] = flat[pl.ds(first + q, side, stride=step), :].astype(BF16)


def pack(core, a_ref, dy_ref, kz, ko, flat, stage, keep, send):
    def put(grad, piece):
        first, side, step = piece
        for q in range(step):
            flat[pl.ds(first + q, side, stride=step), :] = grad[:, q * LANES : (q + 1) * LANES]

    p0, pr, pi = pieces(kz, ko)
    put(mm_at(a_ref[:, :kz], dy_ref[:, :kz]), p0)
    ap = a_ref[:, kz : kz + ko]
    am = a_ref[:, kz + ko :]
    dp = dy_ref[:, kz : kz + ko]
    dm = dy_ref[:, kz + ko :]
    put(mm_at(ap, dp) + mm_at(am, dm), pr)
    put(mm_at(ap, dm) - mm_at(am, dp), pi)
    groups, rows, _ = keep.shape
    part = rows // 4
    for g in range(groups):
        for c in range(2):
            for zh in range(4):
                at = chunk_at(g, c, zh) * part
                stage[c, zh * part : (zh + 1) * part] = flat[at : at + part]
        v0, v1 = stage[0], stage[1]
        keep[g] = jnp.where(core == 0, v0, v1).astype(BF16)
        send[g] = jnp.where(core == 0, v1, v0).astype(BF16)


def first_kernel(nat, core_ref, mine, other, a_ref, x_ref, dt_ref, out_ref, h_ref, flat, stage, w0, wr, wi, m_ref):
    unpack(core_ref[0], mine, other, flat, stage, (w0, wr, wi))
    mix(a_ref, w0, wr, wi, m_ref)
    out = x_ref[...].astype(F32) + back_to_nodes(dt_ref, m_ref, x_ref.shape[1]) / AVG
    out_ref[...] = out
    h_ref[...] = gate(out, nat).astype(BF16)


def middle_kernel(nat, core_ref, mine, other, out_ref, h_ref, cot_ref, rad_ref, b_ref, bt_ref, d_ref, dt_ref,
                  keep, send, dy0_ref, flat, stage, w0, wr, wi, a_ref, m_ref, dy_ref):
    chan = h_ref.shape[1]
    rows = b_ref.shape[0]
    kz, ko = w0.shape[0], wr.shape[0]
    rad = rad_ref[...].astype(F32)
    h1 = h_ref[...]
    rotate(b_ref, h1, rad, a_ref)
    unpack(core_ref[0], mine, other, flat, stage, (w0, wr, wi))
    mix(a_ref, w0, wr, wi, m_ref)
    out2 = h1.astype(F32) + back_to_nodes(dt_ref, m_ref, chan) / AVG
    dout2 = gate_back(cot_ref[...].astype(F32), out2, nat)
    dagg = (dout2 / AVG).astype(BF16)
    for k in range(rows):
        dy_ref[:, k * chan : (k + 1) * chan] = mm(d_ref[k], dagg).astype(BF16)
    pack(core_ref[0], a_ref, dy_ref, kz, ko, flat, stage, keep, send)
    dp = dy_ref[:, kz : kz + ko]
    dm = dy_ref[:, kz + ko :]
    parts = (
        mm_bt(dy_ref[:, :kz], w0[...]),
        mm_bt(dp, wr[...]) + mm_bt(dm, wi[...]),
        mm_bt(dm, wr[...]) - mm_bt(dp, wi[...]),
    )
    at = 0
    for part in parts:
        for q in range(part.shape[1] // chan):
            piece = part[:, q * chan : (q + 1) * chan].astype(BF16).astype(F32)
            m_ref[:, at : at + chan] = (piece * rad).astype(BF16)
            at += chan
    dh1 = (dout2 + back_to_nodes(bt_ref, m_ref, chan)).astype(BF16).astype(F32)
    dagg1 = (gate_back(dh1, out_ref[...], nat) / AVG).astype(BF16)
    for k in range(rows):
        dy0_ref[:, k * chan : (k + 1) * chan] = mm(d_ref[k], dagg1).astype(BF16)


def last_kernel(kz, ko, core_ref, a_ref, dy_ref, keep, send, flat, stage):
    pack(core_ref[0], a_ref, dy_ref, kz, ko, flat, stage, keep, send)


def sds(shape, dtype):
    return jax.ShapeDtypeStruct(shape, dtype)


def call(kernel, outs, args, scratch=(), scalars=0, flops=1 << 32, vmem=28 << 20):
    specs = [pl.BlockSpec(memory_space=pltpu.SMEM)] * scalars
    specs += [pl.BlockSpec(memory_space=pltpu.VMEM)] * (len(args) - scalars)
    return pl.pallas_call(
        kernel,
        out_shape=outs,
        in_specs=specs,
        out_specs=[pl.BlockSpec(memory_space=pltpu.VMEM)] * len(outs),
        scratch_shapes=scratch,
        compiler_params=pltpu.CompilerParams(vmem_limit_bytes=vmem),
        cost_estimate=pl.CostEstimate(flops=flops, bytes_accessed=1 << 20, transcendentals=0),
    )(*args)


def count_of(axes):
    n = 1
    for a in axes:
        n *= lax.axis_size(a)
    return n


def from_everyone(x, axes):
    spread = jnp.broadcast_to(x[None], (count_of(axes), *x.shape))
    return lax.all_to_all(spread, axes, 0, 0, tiled=True)


def swap_core(x):
    return lax.ppermute(x, "core", [(0, 1), (1, 0)])


def local(node_feats, cotangent, wigner, radial, edge_src, edge_dst, edge_count, params, moment1, moment2):
    nat, coef, chan = node_feats.shape
    rows, _, edges = wigner.shape
    lone = (rows + 2) // 3
    kz, ko = lone * chan, (lone - 1) * chan
    layers, shard = params.shape
    far, near = count_of(FAR), count_of(NEAR)
    core = lax.axis_index("core").astype(jnp.int32).reshape(1)
    block = far * shard // LANES

    got = from_everyone(params.astype(BF16), FAR)
    got = jnp.moveaxis(got, 1, 0).reshape(layers, block, LANES)
    mine = [from_everyone(got[i], NEAR) for i in range(layers)]
    other = [swap_core(m) for m in mine]

    x = jnp.transpose(node_feats, (1, 0, 2)).reshape(coef * nat, chan)
    cot = jnp.transpose(cotangent, (1, 0, 2)).reshape(coef * nat, chan)
    live = jnp.arange(edges, dtype=jnp.int32) < edge_count[0]
    dst = jnp.where(live, edge_dst, -1)
    wide = coef * nat
    mats = [sds((rows, edges, wide), BF16), sds((rows, wide, edges), BF16)] * 2
    act = sds((edges, rows * chan), BF16)
    a0, b, bt, d, dt = call(
        functools.partial(prep_kernel, nat),
        [act, *mats],
        (wigner, edge_src.reshape(1, edges), dst.reshape(1, edges), edge_src.reshape(edges, 1), dst.reshape(edges, 1), x, radial[0]),
        vmem=40 << 20,
    )
    flat = [pltpu.VMEM((kz * kz // LANES + 2 * ko * ko // LANES, LANES), F32), pltpu.VMEM((2, block, LANES), F32)]
    weights = [pltpu.VMEM((kz, kz), BF16), pltpu.VMEM((ko, ko), BF16), pltpu.VMEM((ko, ko), BF16)]
    space = pltpu.VMEM((edges, rows * chan), BF16)
    out1, h1 = call(
        functools.partial(first_kernel, nat),
        [sds((wide, chan), F32), sds((wide, chan), BF16)],
        (core, mine[0], other[0], a0, x, dt),
        [*flat, *weights, space],
        scalars=1,
    )
    halves = [sds((near, block, LANES), BF16)] * 2
    keep1, send1, dy0 = call(
        functools.partial(middle_kernel, nat),
        [*halves, act],
        (core, mine[1], other[1], out1, h1, cot, radial[1], b, bt, d, dt),
        [*flat, *weights, space, space, space],
        scalars=1,
        vmem=48 << 20,
    )
    keep0, send0 = call(
        functools.partial(last_kernel, kz, ko), halves, (core, a0, dy0), flat, scalars=1
    )

    def reduce_near(keep, send):
        pair = (keep.astype(F32) + swap_core(send).astype(F32)).astype(BF16)
        arrived = lax.all_to_all(pair, NEAR, 0, 0, tiled=True)
        return arrived.astype(F32).sum(axis=0)

    near1 = reduce_near(keep1, send1)
    near0 = reduce_near(keep0, send0)
    both = jnp.stack([near0, near1]).reshape(layers, far, shard)
    arrived = lax.all_to_all(jnp.moveaxis(both, 0, 1), FAR, 0, 0, tiled=True)
    grad = arrived.sum(axis=0)

    new_moment1 = 0.9 * moment1 + 0.1 * grad
    new_moment2 = 0.95 * moment2 + 0.05 * grad * grad
    m_hat = new_moment1 / (1.0 - 0.9**60)
    v_hat = new_moment2 / (1.0 - 0.95**60)
    new_params = params - 0.01 * (m_hat / (jnp.sqrt(v_hat) + 1e-08) + 0.1 * params)
    return (new_params, new_moment1, new_moment2)


def solution(mesh):
    fine = Mesh(mesh.devices.reshape(SIZES), AXES)
    flat = P(None, AXES)
    return jax.shard_map(
        local,
        mesh=fine,
        in_specs=(
            P(AXES, None, None),
            P(AXES, None, None),
            P(None, None, AXES),
            P(None, AXES, None),
            P(AXES),
            P(AXES),
            P(AXES),
            flat,
            flat,
            flat,
        ),
        out_specs=(flat, flat, flat),
        check_vma=False,
    )
```

profile of v0, /device:TPU:4, one launch (start us, length us, event | category | flops | bytes accessed | tf_op | source)
XLA Modules:
  0.0 153.1 jit_solution(13586705508811123154)
XLA Ops:
  1.5 21.7 %all_to_all.30 = bf16[16,2,3648]{2,1,0:T(2,128)(2,1)S(1)} all-to-all(bf16[16,2,3648]{2,1,0:T(2,128)(2,1)S(1)} %broadcast_in_dim.25), channel_id=1, replica_groups=mesh['zh'=4,'y'=4,'core'=2,'zl'=2,'x'=4] {'zh','x'}, dimensions={0} | all-to-all | bytes 466944 | tf_op jit(solution)/shard_map/all_to_all | solution.py:228
  23.2 1.0 slice_reduce_fusion
  24.4 1.1 broadcast_in_dim.29
  25.5 4.6 %all-to-all-start.2 = ((bf16[8,456,128]{2,1,0:T(8,128)(2,1)}), bf16[8,456,128]{2,1,0:T(8,128)(2,1)S(1)}, u32[]{:S(2)}, u32[]{:S(2)}) async-start(bf16[8,456,128]{2,1,0:T(8,128)(2,1)} %broadcast_in_dim.29), calls=%async_computation.2 | async-start | bytes 1867776 | tf_op jit(solution)/shard_map/all_to_all | solution.py:228
  30.3 12.0 %all-to-all-done.2.mine = bf16[8,456,128]{2,1,0:T(8,128)(2,1)S(1)} async-done(((bf16[8,456,128]{2,1,0:T(8,128)(2,1)}), bf16[8,456,128]{2,1,0:T(8,128)(2,1)S(1)}, u32[]{:S(2)}, u32[]{:S(2)}) %all-to-all-start.2) | async-done | bytes 933920 | tf_op jit(solution)/shard_map/all_to_all | solution.py:228
  42.3 1.1 broadcast_in_dim.27
  43.4 3.6 %all-to-all-start.1 = ((bf16[8,456,128]{2,1,0:T(8,128)(2,1)}), bf16[8,456,128]{2,1,0:T(8,128)(2,1)S(1)}, u32[]{:S(2)}, u32[]{:S(2)}) async-start(bf16[8,456,128]{2,1,0:T(8,128)(2,1)} %broadcast_in_dim.27), calls=%async_computation.1 | async-start | bytes 1867776 | tf_op jit(solution)/shard_map/all_to_all | solution.py:228
  48.0 1.0 copy.20.wig_ref
  49.0 9.9 %all-to-all-done.1.mine = bf16[8,456,128]{2,1,0:T(8,128)(2,1)S(1)} async-done(((bf16[8,456,128]{2,1,0:T(8,128)(2,1)}), bf16[8,456,128]{2,1,0:T(8,128)(2,1)S(1)}, u32[]{:S(2)}, u32[]{:S(2)}) %all-to-all-start.1) | async-done | bytes 933920 | tf_op jit(solution)/shard_map/all_to_all | solution.py:228
  58.9 0.9 slice_bitcast_fusion
  59.8 5.7 %shard_map.121 = (bf16[256,1664]{1,0:T(8,128)(2,1)S(1)}, bf16[13,256,600]{2,1,0:T(8,128)(2,1)S(1)}, bf16[13,600,256]{2,1,0:T(8,128)(2,1)S(1)}, bf16[13,256,600]{2,1,0:T(8,128)(2,1)}, bf16[13,600,256]{2,1,0:T(8,128)(2,1)S(1)}) custom-call(bf16[13,25,256]{2,1,0:T(8,128)(2,1)S(1)} %copy.20.wig_ref, s32[1,256]{1,0:T(1,128)S(1)} %bitcast.24, ...), custom_call_target="tpu_custom_call" | custom-call | flops 4294967296 | bytes 1048576 | tf_op jit(solution)/shard_map/pallas_call | solution.py:208
  65.5 2.6 %shard_map.122 = (f32[600,128]{1,0:T(8,128)S(1)}, bf16[600,128]{1,0:T(8,128)(2,1)S(1)}) custom-call(s32[1]{0:T(128)} %bitcast.core_ref, bf16[8,456,128]{2,1,0:T(8,128)(2,1)S(1)} %all-to-all-done.2.mine, bf16[8,456,128]{2,1,0:T(8,128)(2,1)S(1)} %collective-permute-done.1.other, bf16[256,1664]{1,0:T(8,128)(2,1)S(1)} %get-tuple-element.15.a_ref, ...), custom_call_target="tpu_custom_call" | custom-call | flops 4294967296 | bytes 1048576 | tf_op jit(solution)/shard_map/pallas_call | solution.py:208
  68.7 1.2 copy-done.2
  69.9 17.5 %shard_map.123 = (bf16[8,456,128]{2,1,0:T(8,128)(2,1)S(1)}, bf16[8,456,128]{2,1,0:T(8,128)(2,1)S(1)}, bf16[256,1664]{1,0:T(8,128)(2,1)S(1)}) custom-call(s32[1]{0:T(128)} %bitcast.core_ref, bf16[8,456,128]{2,1,0:T(8,128)(2,1)S(1)} %all-to-all-done.1.mine, bf16[8,456,128]{2,1,0:T(8,128)(2,1)S(1)} %collective-permute-done.other, ...), custom_call_target="tpu_custom_call" | custom-call | flops 4294967296 | bytes 1048576 | tf_op jit(solution)/shard_map/pallas_call | solution.py:208
  87.4 1.3 shard_map.124
  89.3 2.1 %collective-permute-done.2 = bf16[8,456,128]{2,1,0:T(8,128)(2,1)S(1)} collective-permute-done((bf16[8,456,128]{2,1,0:T(8,128)(2,1)S(1)}, bf16[8,456,128]{2,1,0:T(8,128)(2,1)S(1)}, u32[]{:S(2)}, u32[]{:S(2)}) %collective-permute-start.2) | collective-permute-done | bytes 933920 | tf_op jit(solution)/shard_map/ppermute | solution.py:232
  91.4 1.2 add_convert_fusion.1
  92.7 3.6 %all-to-all-start.3 = ((bf16[8,456,128]{2,1,0:T(8,128)(2,1)}), bf16[8,456,128]{2,1,0:T(8,128)(2,1)S(1)}, u32[]{:S(2)}, u32[]{:S(2)}) async-start(bf16[8,456,128]{2,1,0:T(8,128)(2,1)} %add_convert_fusion.1), calls=%async_computation.3 | async-start | bytes 1867776 | tf_op jit(solution)/shard_map/all_to_all | solution.py:288
  96.7 2.1 %collective-permute-done.3 = bf16[8,456,128]{2,1,0:T(8,128)(2,1)S(1)} collective-permute-done((bf16[8,456,128]{2,1,0:T(8,128)(2,1)S(1)}, bf16[8,456,128]{2,1,0:T(8,128)(2,1)S(1)}, u32[]{:S(2)}, u32[]{:S(2)}) %collective-permute-start.3) | collective-permute-done | bytes 933920 | tf_op jit(solution)/shard_map/ppermute | solution.py:232
  98.8 1.2 add_convert_fusion
  100.0 11.5 %all-to-all-done.3 = bf16[8,456,128]{2,1,0:T(8,128)(2,1)S(1)} async-done(((bf16[8,456,128]{2,1,0:T(8,128)(2,1)}), bf16[8,456,128]{2,1,0:T(8,128)(2,1)S(1)}, u32[]{:S(2)}, u32[]{:S(2)}) %all-to-all-start.3) | async-done | bytes 933920 | tf_op jit(solution)/shard_map/all_to_all | solution.py:288
  111.5 3.6 %all-to-all-start.4 = ((bf16[8,456,128]{2,1,0:T(8,128)(2,1)}), bf16[8,456,128]{2,1,0:T(8,128)(2,1)S(1)}, u32[]{:S(2)}, u32[]{:S(2)}) async-start(bf16[8,456,128]{2,1,0:T(8,128)(2,1)} %add_convert_fusion), calls=%async_computation.4 | async-start | bytes 1867776 | tf_op jit(solution)/shard_map/all_to_all | solution.py:288
  115.5 13.9 %all-to-all-done.4 = bf16[8,456,128]{2,1,0:T(8,128)(2,1)S(1)} async-done(((bf16[8,456,128]{2,1,0:T(8,128)(2,1)}), bf16[8,456,128]{2,1,0:T(8,128)(2,1)S(1)}, u32[]{:S(2)}, u32[]{:S(2)}) %all-to-all-start.4) | async-done | bytes 933920 | tf_op jit(solution)/shard_map/all_to_all | solution.py:288
  130.3 21.9 %all_to_all.31 = f32[16,2,3648]{2,1,0:T(2,128)S(1)} all-to-all(f32[16,2,3648]{2,1,0:T(2,128)S(1)} %maximum_bitcast_fusion), channel_id=1, replica_groups=mesh['zh'=4,'y'=4,'core'=2,'zl'=2,'x'=4] {'zh','x'}, dimensions={0} | all-to-all | bytes 933888 | tf_op jit(solution)/shard_map/all_to_all | solution.py:294
  (39 shorter events, 5.4 us)
Async XLA Ops:
  25.5 16.8 %all-to-all-start.2 = ((bf16[8,456,128]{2,1,0:T(8,128)(2,1)}), bf16[8,456,128]{2,1,0:T(8,128)(2,1)S(1)}, u32[]{:S(2)}, u32[]{:S(2)}) async-start(bf16[8,456,128]{2,1,0:T(8,128)(2,1)} %broadcast_in_dim.29), calls=%async_computation.2 | async-start | bytes 1867776 | tf_op jit(solution)/shard_map/all_to_all | solution.py:228
  30.1 17.6 %copy-start.9 = (s32[256]{0:T(256)S(1)}, s32[256]{0:T(256)}, u32[]{:S(2)}) copy-start(s32[256]{0:T(256)} %param.15) | copy-start | bytes 3076
  30.1 17.8 %copy-start.4 = (s32[256]{0:T(256)S(1)}, s32[256]{0:T(256)}, u32[]{:S(2)}) copy-start(s32[256]{0:T(256)} %param.14) | copy-start | bytes 3076
  30.3 29.5 %copy-start.5 = (bf16[24,25,128]{2,0,1:T(8,128)(2,1)S(1)}, bf16[24,25,128]{2,0,1:T(8,128)(2,1)}, u32[]{:S(2)}) copy-start(bf16[24,25,128]{2,0,1:T(8,128)(2,1)} %param.10) | copy-start | bytes 460804
  43.4 15.5 %all-to-all-start.1 = ((bf16[8,456,128]{2,1,0:T(8,128)(2,1)}), bf16[8,456,128]{2,1,0:T(8,128)(2,1)S(1)}, u32[]{:S(2)}, u32[]{:S(2)}) async-start(bf16[8,456,128]{2,1,0:T(8,128)(2,1)} %broadcast_in_dim.27), calls=%async_computation.1 | async-start | bytes 1867776 | tf_op jit(solution)/shard_map/all_to_all | solution.py:228
  47.0 18.6 %collective-permute-start.1 = (bf16[8,456,128]{2,1,0:T(8,128)(2,1)S(1)}, bf16[8,456,128]{2,1,0:T(8,128)(2,1)S(1)}, u32[]{:S(2)}, u32[]{:S(2)}) collective-permute-start(bf16[8,456,128]{2,1,0:T(8,128)(2,1)S(1)} %all-to-all-done.2.mine), channel_id=1, source_target_pairs={{0,8},{8,0},{1,9},{9,1},{2,10},{10,2},{3,11},{11,3},{4,12},{12,4},... | collective-permute-start | bytes 2801672 | tf_op jit(solution)/shard_map/ppermute | solution.py:232
  58.9 11.0 %collective-permute-start = (bf16[8,456,128]{2,1,0:T(8,128)(2,1)S(1)}, bf16[8,456,128]{2,1,0:T(8,128)(2,1)S(1)}, u32[]{:S(2)}, u32[]{:S(2)}) collective-permute-start(bf16[8,456,128]{2,1,0:T(8,128)(2,1)S(1)} %all-to-all-done.1.mine), channel_id=1, source_target_pairs={{0,8},{8,0},{1,9},{9,1},{2,10},{10,2},{3,11},{11,3},{4,12},{12,4},... | collective-permute-start | bytes 2801672 | tf_op jit(solution)/shard_map/ppermute | solution.py:232
  65.5 2.7 %copy-start = (bf16[13,256,600]{2,1,0:T(8,128)(2,1)}, bf16[13,256,600]{2,1,0:T(8,128)(2,1)S(1)}, u32[]{:S(2)}) copy-start(bf16[13,256,600]{2,1,0:T(8,128)(2,1)S(1)} %get-tuple-element.19.b_ref) | copy-start | bytes 11980804
  65.5 3.2 %copy-start.1 = (bf16[13,600,256]{2,1,0:T(8,128)(2,1)}, bf16[13,600,256]{2,1,0:T(8,128)(2,1)S(1)}, u32[]{:S(2)}) copy-start(bf16[13,600,256]{2,1,0:T(8,128)(2,1)S(1)} %get-tuple-element.20.bt_ref) | copy-start | bytes 11980804
  65.5 4.4 %copy-start.2 = (bf16[13,600,256]{2,1,0:T(8,128)(2,1)}, bf16[13,600,256]{2,1,0:T(8,128)(2,1)S(1)}, u32[]{:S(2)}) copy-start(bf16[13,600,256]{2,1,0:T(8,128)(2,1)S(1)} %get-tuple-element.16.dt_ref) | copy-start | bytes 11980804
  65.5 4.4 %copy-start.3 = (bf16[24,25,128]{2,0,1:T(8,128)(2,1)S(1)}, bf16[24,25,128]{2,0,1:T(8,128)(2,1)}, u32[]{:S(2)}) copy-start(bf16[24,25,128]{2,0,1:T(8,128)(2,1)} %param.11) | copy-start | bytes 460804
  88.7 2.7 %collective-permute-start.2 = (bf16[8,456,128]{2,1,0:T(8,128)(2,1)S(1)}, bf16[8,456,128]{2,1,0:T(8,128)(2,1)S(1)}, u32[]{:S(2)}, u32[]{:S(2)}) collective-permute-start(bf16[8,456,128]{2,1,0:T(8,128)(2,1)S(1)} %get-tuple-element.24), channel_id=1, source_target_pairs={{0,8},{8,0},{1,9},{9,1},{2,10},{10,2},{3,11},{11,3},{4,12},{12,4},... | collective-permute-start | bytes 2801672 | tf_op jit(solution)/shard_map/ppermute | solution.py:232
  92.7 18.8 %all-to-all-start.3 = ((bf16[8,456,128]{2,1,0:T(8,128)(2,1)}), bf16[8,456,128]{2,1,0:T(8,128)(2,1)S(1)}, u32[]{:S(2)}, u32[]{:S(2)}) async-start(bf16[8,456,128]{2,1,0:T(8,128)(2,1)} %add_convert_fusion.1), calls=%async_computation.3 | async-start | bytes 1867776 | tf_op jit(solution)/shard_map/all_to_all | solution.py:288
  96.2 2.6 %collective-permute-start.3 = (bf16[8,456,128]{2,1,0:T(8,128)(2,1)S(1)}, bf16[8,456,128]{2,1,0:T(8,128)(2,1)S(1)}, u32[]{:S(2)}, u32[]{:S(2)}) collective-permute-start(bf16[8,456,128]{2,1,0:T(8,128)(2,1)S(1)} %get-tuple-element.26), channel_id=1, source_target_pairs={{0,8},{8,0},{1,9},{9,1},{2,10},{10,2},{3,11},{11,3},{4,12},{12,4},... | collective-permute-start | bytes 2801672 | tf_op jit(solution)/shard_map/ppermute | solution.py:232
  111.5 17.9 %all-to-all-start.4 = ((bf16[8,456,128]{2,1,0:T(8,128)(2,1)}), bf16[8,456,128]{2,1,0:T(8,128)(2,1)S(1)}, u32[]{:S(2)}, u32[]{:S(2)}) async-start(bf16[8,456,128]{2,1,0:T(8,128)(2,1)} %add_convert_fusion), calls=%async_computation.4 | async-start | bytes 1867776 | tf_op jit(solution)/shard_map/all_to_all | solution.py:288
  115.5 36.8 %copy-start.6 = (f32[2,3648]{1,0:T(2,128)S(1)}, f32[2,3648]{1,0:T(2,128)}, u32[]{:S(2)}) copy-start(f32[2,3648]{1,0:T(2,128)} %param.17) | copy-start | bytes 87556
  115.5 36.8 %copy-start.7 = (f32[2,3648]{1,0:T(2,128)S(1)}, f32[2,3648]{1,0:T(2,128)}, u32[]{:S(2)}) copy-start(f32[2,3648]{1,0:T(2,128)} %param.18) | copy-start | bytes 87556
  115.5 36.8 %copy-start.8 = (f32[2,3648]{1,0:T(2,128)S(1)}, f32[2,3648]{1,0:T(2,128)}, u32[]{:S(2)}) copy-start(f32[2,3648]{1,0:T(2,128)} %param.19) | copy-start | bytes 87556
where the time goes:
time: 154 us; the launch traced here: 153 us
  waiting for transfers between devices  51.5 us (33%)
  blocking collectives  43.6 us (28%)
  Pallas kernels  27.2 us (18%)
  starting transfers between devices  16.4 us (11%)
  local copies, waits for them, and re-layouts  8.07 us (5%)
  other arithmetic  4.76 us (3%)
    pallas_call x4, Pallas kernels, call(): pl.pallas_call(kernel, out_shape=outs, in_specs=specs, out_specs=[pl.Bloc...  27.2 us
    all_to_all x2, waiting for transfers between devices, reduce_near(): arrived = lax.all_to_all(pair, NEAR, 0, 0, tiled=True)  25.4 us
    all_to_all x2, waiting for transfers between devices, from_everyone(): return lax.all_to_all(spread, axes, 0, 0, tiled=True)  21.9 us
    all_to_all x1, blocking collectives, local(): arrived = lax.all_to_all(jnp.moveaxis(both, 0, 1), FAR, 0, 0, tiled=True)  21.9 us
    all_to_all x1, blocking collectives, from_everyone(): return lax.all_to_all(spread, axes, 0, 0, tiled=True)  21.7 us
    all_to_all x2, starting transfers between devices, from_everyone(): return lax.all_to_all(spread, axes, 0, 0, tiled=True)  8.17 us
    all_to_all x2, starting transfers between devices, reduce_near(): arrived = lax.all_to_all(pair, NEAR, 0, 0, tiled=True)  7.1 us
    ppermute x4, waiting for transfers between devices, swap_core(): return lax.ppermute(x, 'core', [(0, 1), (1, 0)])  4.25 us
  transfers between devices with their start and end apart: 8, of which 6 were waited for; matrix products, arithmetic and copies ran while one was open for 3% of the time, Pallas kernels for 5%

commit v1 on v0

--- a/solution.py
+++ b/solution.py
@@ -13,8 +13,8 @@
 AVG = 10
 AXES = ("zh", "y", "core", "zl", "x")
 SIZES = (4, 4, 2, 2, 4)
-NEAR = ("y", "zl")
-FAR = ("zh", "x")
+NEAR = ("y", "zl", "x")
+FAR = ("zh",)
 LANES = 128
 
 
@@ -104,32 +104,50 @@
     return ((0, kz, kz // LANES), (first, ko, ko // LANES), (second, ko, ko // LANES))
 
 
-def chunk_at(g, core, zh):
-    y, zl = divmod(g, 2)
-    return ((zh * 4 + y) * 2 + core) * 2 + zl
-
-
-def unpack(core, mine, other, flat, stage, weights):
-    groups, rows, _ = mine.shape
-    part = rows // 4
-    for g in range(groups):
+def chunks(core):
+    zhs, ys, cores, zls, xs = SIZES
+    for y in range(ys):
+        for zl in range(zls):
+            for x in range(xs):
+                for zh in range(zhs):
+                    owner = (((zh * ys + y) * cores + core) * zls + zl) * xs + x
+                    yield owner // 2, owner % 2, (y * zls + zl) * xs + x, zh
+
+
+def unpack(core, mine, other, flat, stage):
+    layers = flat.shape[0]
+    part = stage.shape[1] // (SIZES[0] * layers)
+    pair = 2 * part - 1
+    where = [list(chunks(c)) for c in range(2)]
+    first = lax.broadcasted_iota(jnp.int32, (part, LANES), 0) == 0
+    for g in range(mine.shape[0]):
         m = mine[g].astype(F32)
         o = other[g].astype(F32)
         for c in range(2):
             stage[c] = jnp.where(core == c, m, o)
-            for zh in range(4):
-                at = chunk_at(g, c, zh) * part
-                flat[at : at + part] = stage[c, zh * part : (zh + 1) * part]
+            for row, odd, sender, zh in where[c]:
+                if sender != g:
+                    continue
+                for i in range(layers):
+                    at = (zh * layers + i) * part
+                    block = stage[c, at : at + part]
+                    to = row * pair + odd * (part - 1)
+                    if odd:
+                        block = jnp.where(first, block + flat[i, to : to + part], block)
+                    flat[i, to : to + part] = block
+
+
+def take_weights(flat, layer, weights):
     for ref, (first, side, step) in zip(weights, pieces(weights[0].shape[0], weights[1].shape[0])):
         for q in range(step):
-            ref[:, q * LANES : (q + 1) * LANES] = flat[pl.ds(first + q, side, stride=step), :].astype(BF16)
-
-
-def pack(core, a_ref, dy_ref, kz, ko, flat, stage, keep, send):
+            ref[:, q * LANES : (q + 1) * LANES] = flat[layer, pl.ds(first + q, side, stride=step), :].astype(BF16)
+
+
+def put_grads(a_ref, dy_ref, kz, ko, layer, flat):
     def put(grad, piece):
         first, side, step = piece
         for q in range(step):
-            flat[pl.ds(first + q, side, stride=step), :] = grad[:, q * LANES : (q + 1) * LANES]
+            flat[layer, pl.ds(first + q, side, stride=step), :] = grad[:, q * LANES : (q + 1) * LANES]
 
     p0, pr, pi = pieces(kz, ko)
     put(mm_at(a_ref[:, :kz], dy_ref[:, :kz]), p0)
@@ -139,42 +157,57 @@
     dm = dy_ref[:, kz + ko :]
     put(mm_at(ap, dp) + mm_at(am, dm), pr)
     put(mm_at(ap, dm) - mm_at(am, dp), pi)
-    groups, rows, _ = keep.shape
-    part = rows // 4
-    for g in range(groups):
+
+
+def pack(core, flat, stage, keep, send):
+    layers = flat.shape[0]
+    part = stage.shape[1] // (SIZES[0] * layers)
+    pair = 2 * part - 1
+    where = [list(chunks(c)) for c in range(2)]
+    for g in range(keep.shape[0]):
         for c in range(2):
-            for zh in range(4):
-                at = chunk_at(g, c, zh) * part
-                stage[c, zh * part : (zh + 1) * part] = flat[at : at + part]
+            for row, odd, sender, zh in where[c]:
+                if sender != g:
+                    continue
+                for i in range(layers):
+                    at = (zh * layers + i) * part
+                    to = row * pair + odd * (part - 1)
+                    stage[c, at : at + part] = flat[i, to : to + part]
         v0, v1 = stage[0], stage[1]
         keep[g] = jnp.where(core == 0, v0, v1).astype(BF16)
         send[g] = jnp.where(core == 0, v1, v0).astype(BF16)
 
 
-def first_kernel(nat, core_ref, mine, other, a_ref, x_ref, dt_ref, out_ref, h_ref, flat, stage, w0, wr, wi, m_ref):
-    unpack(core_ref[0], mine, other, flat, stage, (w0, wr, wi))
-    mix(a_ref, w0, wr, wi, m_ref)
-    out = x_ref[...].astype(F32) + back_to_nodes(dt_ref, m_ref, x_ref.shape[1]) / AVG
-    out_ref[...] = out
-    h_ref[...] = gate(out, nat).astype(BF16)
-
-
-def middle_kernel(nat, core_ref, mine, other, out_ref, h_ref, cot_ref, rad_ref, b_ref, bt_ref, d_ref, dt_ref,
-                  keep, send, dy0_ref, flat, stage, w0, wr, wi, a_ref, m_ref, dy_ref):
-    chan = h_ref.shape[1]
+def main_kernel(nat, core_ref, mine, other, a0_ref, x_ref, cot_ref, rad_ref, b_far, bt_far, d_far, dt_far,
+                keep, send, flat, stage, w0, wr, wi, a_ref, m_ref, dy_ref, b_ref, bt_ref, d_ref, dt_ref, sems):
+    moves = [
+        pltpu.make_async_copy(far, near, sems.at[i])
+        for i, (far, near) in enumerate(((dt_far, dt_ref), (b_far, b_ref), (d_far, d_ref), (bt_far, bt_ref)))
+    ]
+    for move in moves:
+        move.start()
+    chan = x_ref.shape[1]
     rows = b_ref.shape[0]
     kz, ko = w0.shape[0], wr.shape[0]
+    core = core_ref[0]
     rad = rad_ref[...].astype(F32)
-    h1 = h_ref[...]
+    unpack(core, mine, other, flat, stage)
+    take_weights(flat, 0, (w0, wr, wi))
+    mix(a0_ref, w0, wr, wi, m_ref)
+    moves[0].wait()
+    out1 = x_ref[...].astype(F32) + back_to_nodes(dt_ref, m_ref, chan) / AVG
+    h1 = gate(out1, nat).astype(BF16)
+    moves[1].wait()
     rotate(b_ref, h1, rad, a_ref)
-    unpack(core_ref[0], mine, other, flat, stage, (w0, wr, wi))
+    take_weights(flat, 1, (w0, wr, wi))
     mix(a_ref, w0, wr, wi, m_ref)
     out2 = h1.astype(F32) + back_to_nodes(dt_ref, m_ref, chan) / AVG
     dout2 = gate_back(cot_ref[...].astype(F32), out2, nat)
     dagg = (dout2 / AVG).astype(BF16)
+    moves[2].wait()
     for k in range(rows):
         dy_ref[:, k * chan : (k + 1) * chan] = mm(d_ref[k], dagg).astype(BF16)
-    pack(core_ref[0], a_ref, dy_ref, kz, ko, flat, stage, keep, send)
+    put_grads(a_ref, dy_ref, kz, ko, 1, flat)
     dp = dy_ref[:, kz : kz + ko]
     dm = dy_ref[:, kz + ko :]
     parts = (
@@ -188,23 +221,23 @@
             piece = part[:, q * chan : (q + 1) * chan].astype(BF16).astype(F32)
             m_ref[:, at : at + chan] = (piece * rad).astype(BF16)
             at += chan
+    moves[3].wait()
     dh1 = (dout2 + back_to_nodes(bt_ref, m_ref, chan)).astype(BF16).astype(F32)
-    dagg1 = (gate_back(dh1, out_ref[...], nat) / AVG).astype(BF16)
+    dagg1 = (gate_back(dh1, out1, nat) / AVG).astype(BF16)
     for k in range(rows):
-        dy0_ref[:, k * chan : (k + 1) * chan] = mm(d_ref[k], dagg1).astype(BF16)
-
-
-def last_kernel(kz, ko, core_ref, a_ref, dy_ref, keep, send, flat, stage):
-    pack(core_ref[0], a_ref, dy_ref, kz, ko, flat, stage, keep, send)
+        dy_ref[:, k * chan : (k + 1) * chan] = mm(d_ref[k], dagg1).astype(BF16)
+    put_grads(a0_ref, dy_ref, kz, ko, 0, flat)
+    pack(core, flat, stage, keep, send)
 
 
 def sds(shape, dtype):
     return jax.ShapeDtypeStruct(shape, dtype)
 
 
-def call(kernel, outs, args, scratch=(), scalars=0, flops=1 << 32, vmem=28 << 20):
+def call(kernel, outs, args, scratch=(), scalars=0, far=0, flops=1 << 32, vmem=28 << 20):
     specs = [pl.BlockSpec(memory_space=pltpu.SMEM)] * scalars
-    specs += [pl.BlockSpec(memory_space=pltpu.VMEM)] * (len(args) - scalars)
+    specs += [pl.BlockSpec(memory_space=pltpu.VMEM)] * (len(args) - scalars - far)
+    specs += [pl.BlockSpec(memory_space=pl.ANY)] * far
     return pl.pallas_call(
         kernel,
         out_shape=outs,
@@ -240,12 +273,15 @@
     layers, shard = params.shape
     far, near = count_of(FAR), count_of(NEAR)
     core = lax.axis_index("core").astype(jnp.int32).reshape(1)
-    block = far * shard // LANES
-
-    got = from_everyone(params.astype(BF16), FAR)
-    got = jnp.moveaxis(got, 1, 0).reshape(layers, block, LANES)
-    mine = [from_everyone(got[i], NEAR) for i in range(layers)]
-    other = [swap_core(m) for m in mine]
+    odd = lax.axis_index("x") % 2 == 1
+    part = (shard + LANES // 2) // LANES
+    spare = part * LANES - shard
+
+    half = params.astype(BF16)
+    half = jnp.where(odd, jnp.pad(half, ((0, 0), (spare, 0))), jnp.pad(half, ((0, 0), (0, spare))))
+    got = from_everyone(half.reshape(layers * part, LANES), FAR).reshape(far * layers * part, LANES)
+    mine = from_everyone(got, NEAR)
+    other = swap_core(mine)
 
     x = jnp.transpose(node_feats, (1, 0, 2)).reshape(coef * nat, chan)
     cot = jnp.transpose(cotangent, (1, 0, 2)).reshape(coef * nat, chan)
@@ -258,41 +294,27 @@
         functools.partial(prep_kernel, nat),
         [act, *mats],
         (wigner, edge_src.reshape(1, edges), dst.reshape(1, edges), edge_src.reshape(edges, 1), dst.reshape(edges, 1), x, radial[0]),
-        vmem=40 << 20,
+        vmem=24 << 20,
     )
-    flat = [pltpu.VMEM((kz * kz // LANES + 2 * ko * ko // LANES, LANES), F32), pltpu.VMEM((2, block, LANES), F32)]
+    block = far * layers * part
+    flat = [pltpu.VMEM((layers, (kz * kz + 2 * ko * ko) // LANES, LANES), F32), pltpu.VMEM((2, block, LANES), F32)]
     weights = [pltpu.VMEM((kz, kz), BF16), pltpu.VMEM((ko, ko), BF16), pltpu.VMEM((ko, ko), BF16)]
     space = pltpu.VMEM((edges, rows * chan), BF16)
-    out1, h1 = call(
-        functools.partial(first_kernel, nat),
-        [sds((wide, chan), F32), sds((wide, chan), BF16)],
-        (core, mine[0], other[0], a0, x, dt),
-        [*flat, *weights, space],
+    held = [pltpu.VMEM(m.shape, m.dtype) for m in mats]
+    keep, send = call(
+        functools.partial(main_kernel, nat),
+        [sds((near, block, LANES), BF16)] * 2,
+        (core, mine, other, a0, x, cot, radial[1], b, bt, d, dt),
+        [*flat, *weights, space, space, space, *held, pltpu.SemaphoreType.DMA((len(held),))],
         scalars=1,
+        far=len(held),
+        vmem=44 << 20,
     )
-    halves = [sds((near, block, LANES), BF16)] * 2
-    keep1, send1, dy0 = call(
-        functools.partial(middle_kernel, nat),
-        [*halves, act],
-        (core, mine[1], other[1], out1, h1, cot, radial[1], b, bt, d, dt),
-        [*flat, *weights, space, space, space],
-        scalars=1,
-        vmem=48 << 20,
-    )
-    keep0, send0 = call(
-        functools.partial(last_kernel, kz, ko), halves, (core, a0, dy0), flat, scalars=1
-    )
-
-    def reduce_near(keep, send):
-        pair = (keep.astype(F32) + swap_core(send).astype(F32)).astype(BF16)
-        arrived = lax.all_to_all(pair, NEAR, 0, 0, tiled=True)
-        return arrived.astype(F32).sum(axis=0)
-
-    near1 = reduce_near(keep1, send1)
-    near0 = reduce_near(keep0, send0)
-    both = jnp.stack([near0, near1]).reshape(layers, far, shard)
-    arrived = lax.all_to_all(jnp.moveaxis(both, 0, 1), FAR, 0, 0, tiled=True)
-    grad = arrived.sum(axis=0)
+    pair = (keep.astype(F32) + swap_core(send).astype(F32)).astype(BF16)
+    arrived = lax.all_to_all(pair, NEAR, 0, 0, tiled=True)
+    near_sum = arrived.astype(F32).sum(axis=0).reshape(far, layers * part, LANES)
+    grad = lax.all_to_all(near_sum, FAR, 0, 0, tiled=True).sum(axis=0).reshape(layers, part * LANES)
+    grad = jnp.where(odd, grad[:, spare:], grad[:, :shard])
 
     new_moment1 = 0.9 * moment1 + 0.1 * grad
     new_moment2 = 0.95 * moment2 + 0.05 * grad * grad

time: 154 us -> 131 us (0.85)
  waiting for transfers between devices: 51.5 us -> 3.51 us
  blocking collectives: 43.6 us -> 90.2 us
  starting transfers between devices: 16.4 us -> 0.6 us
  Pallas kernels: 27.2 us -> 23.9 us
  other arithmetic: 4.76 us -> 2.42 us
    all_to_all x4 -> x0, waiting for transfers between devices: 47.3 us -> none  [the longest x2 25.4 us: reduce_near(): arrived = lax.all_to_all(pair, NEAR, 0, 0, tiled=True)]
    all_to_all x1 -> x2, blocking collectives: 21.7 us -> 47.8 us  [from_everyone(): return lax.all_to_all(spread, axes, 0, 0, tiled=True)]
    all_to_all x1 -> x2, blocking collectives: 21.9 us -> 42.4 us  [the longest x1 31.3 us: local(): arrived = lax.all_to_all(pair, NEAR, 0, 0, tiled=True)]
    all_to_all x4 -> x0, starting transfers between devices: 15.3 us -> none  [the longest x2 8.17 us: from_everyone(): return lax.all_to_all(spread, axes, 0, 0, tiled=True)]
    unnamed x21 -> x27, local copies, waits for them, and re-layouts: 2.75 us -> 7.9 us
    pallas_call x4 -> x2, Pallas kernels: 27.2 us -> 23.9 us  [call(): pl.pallas_call(kernel, out_shape=outs, in_specs=specs, out_specs=[pl.Bloc...]
    broadcast_in_dim x5 -> x4, local copies, waits for them, and re-layouts: 2.59 us -> 0.31 us  [from_everyone(): spread = jnp.broadcast_to(x[None], (count_of(axes), *x.shape))]
    convert_element_type x3 -> x2, other arithmetic: 3.19 us -> 1.26 us  [the longest x1 0.76 us: local(): half = params.astype(BF16)]
  transfers between devices with their start and end apart: 8 -> 2, of which waited for: 6 -> 1; matrix products, arithmetic and copies ran while one was open for 3% -> 0% of each run, Pallas kernels for 5% -> 3%
where the time goes in v1:
time: 131 us
  blocking collectives  90.2 us (69%)
  Pallas kernels  23.9 us (18%)
  local copies, waits for them, and re-layouts  8.52 us (7%)
  waiting for transfers between devices  3.51 us (3%)
  other arithmetic  2.42 us (2%)
  between operations  1.52 us (1%)
    all_to_all x2, blocking collectives, from_everyone(): return lax.all_to_all(spread, axes, 0, 0, tiled=True)  47.8 us
    all_to_all x1, blocking collectives, local(): arrived = lax.all_to_all(pair, NEAR, 0, 0, tiled=True)  31.3 us
    pallas_call x2, Pallas kernels, call(): pl.pallas_call(kernel, out_shape=outs, in_specs=specs, out_specs=[pl.Bloc...  23.9 us
    all_to_all x1, blocking collectives, local(): lax.all_to_all(near_sum, FAR, 0, 0, tiled=True).sum(axis=0)  11.1 us
    unnamed x27, local copies, waits for them, and re-layouts  7.9 us
    ppermute x2, waiting for transfers between devices, swap_core(): return lax.ppermute(x, 'core', [(0, 1), (1, 0)])  3.51 us
  transfers between devices with their start and end apart: 2, of which 1 were waited for; matrix products, arithmetic and copies ran while one was open for 0% of the time, Pallas kernels for 3%

profile of v1, /device:TPU:4, one launch (start us, length us, event | category | flops | bytes accessed | tf_op | source)
XLA Modules:
  0.0 130.7 jit_solution(16087722804830717011)
XLA Ops:
  0.6 0.8 convert_element_type.19
  1.4 0.1 broadcast_select_fusion
  1.6 16.5 %all_to_all.20 = bf16[4,58,128]{2,1,0:T(8,128)(2,1)S(1)} all-to-all(bf16[4,58,128]{2,1,0:T(8,128)(2,1)S(1)} %broadcast_in_dim.19), channel_id=1, replica_groups=mesh['zh'=4,'y'=4,'core'=2,'zl'=2,'x'=4] {'zh'}, dimensions={0} | all-to-all | bytes 118784 | tf_op jit(solution)/shard_map/all_to_all | solution.py:261
  18.0 0.2 broadcast_in_dim.21
  18.3 0.0 copy-start.12
  18.3 0.0 copy-start.6
  18.4 0.0 copy-start.4
  18.4 31.4 %all_to_all.21.mine = bf16[32,232,128]{2,1,0:T(8,128)(2,1)S(1)} all-to-all(bf16[32,232,128]{2,1,0:T(8,128)(2,1)S(1)} %broadcast_in_dim.21), channel_id=1, replica_groups=mesh['zh'=4,'y'=4,'core'=2,'zl'=2,'x'=4] {'y','zl','x'}, dimensions={0} | all-to-all | bytes 3801088 | tf_op jit(solution)/shard_map/all_to_all | solution.py:261
  50.4 0.1 copy.16.dstc_ref
  50.6 0.1 copy.15.srcc_ref
  50.7 0.1 copy.14.wig_ref
  50.8 3.9 %shard_map.121 = (bf16[256,1664]{1,0:T(8,128)(2,1)S(1)}, bf16[13,256,600]{2,1,0:T(8,128)(2,1)S(1)}, bf16[13,600,256]{2,1,0:T(8,128)(2,1)S(1)}, bf16[13,256,600]{...) custom-call(bf16[13,25,256]{2,1,0:T(8,128)(2,1)S(1)} %copy.14.wig_ref, s32[1,256]{1,0:T(1,128)S(1)} %bitcast.23, ...), custom_call_target="tpu_custom_call" | custom-call | flops 4294967296 | bytes 1048576 | tf_op jit(solution)/shard_map/pallas_call | solution.py:241
  54.8 2.0 %copy-done = bf16[13,256,600]{2,1,0:T(8,128)(2,1)} copy-done((bf16[13,256,600]{2,1,0:T(8,128)(2,1)}, bf16[13,256,600]{2,1,0:T(8,128)(2,1)S(1)}, u32[]{:S(2)}) %copy-start) | copy-done | bytes 3993624
  56.8 2.0 %copy-done.1 = bf16[13,256,600]{2,1,0:T(8,128)(2,1)} copy-done((bf16[13,256,600]{2,1,0:T(8,128)(2,1)}, bf16[13,256,600]{2,1,0:T(8,128)(2,1)S(1)}, u32[]{:S(2)}) %copy-start.1) | copy-done | bytes 3993624
  58.8 1.9 %copy-done.2 = bf16[13,600,256]{2,1,0:T(8,128)(2,1)} copy-done((bf16[13,600,256]{2,1,0:T(8,128)(2,1)}, bf16[13,600,256]{2,1,0:T(8,128)(2,1)S(1)}, u32[]{:S(2)}) %copy-start.2) | copy-done | bytes 3993624
  60.7 1.9 %copy-done.3 = bf16[13,600,256]{2,1,0:T(8,128)(2,1)} copy-done((bf16[13,600,256]{2,1,0:T(8,128)(2,1)}, bf16[13,600,256]{2,1,0:T(8,128)(2,1)S(1)}, u32[]{:S(2)}) %copy-start.3) | copy-done | bytes 3993624
  62.6 20.0 %shard_map.122 = (bf16[32,232,128]{2,1,0:T(8,128)(2,1)S(1)}, bf16[32,232,128]{2,1,0:T(8,128)(2,1)S(1)}) custom-call(s32[1]{0:T(128)} %bitcast.core_ref, bf16[32,232,128]{2,1,0:T(8,128)(2,1)S(1)} %all_to_all.21.mine, bf16[32,232,128]{2,1,0:T(8,128)(2,1)} %collective-permute-done.other, bf16[256,1664]{1,0:T(8,128)(2,1)S(1)} %get-tuple-element.10.a0_ref, ...), custom_call_target="tpu_custom_call" | custom-call | flops 4294967296 | bytes 1048576 | tf_op jit(solution)/shard_map/pallas_call | solution.py:241
  82.6 0.6 collective-permute-start.1
  83.2 3.5 %collective-permute-done.1 = bf16[32,232,128]{2,1,0:T(8,128)(2,1)S(1)} collective-permute-done((bf16[32,232,128]{2,1,0:T(8,128)(2,1)S(1)}, bf16[32,232,128]{2,1,0:T(8,128)(2,1)S(1)}, u32[]{:S(2)}, u32[]{:S(2)}) %collective-permute-start.1) | collective-permute-done | bytes 1900576 | tf_op jit(solution)/shard_map/ppermute | solution.py:265
  86.7 0.5 add_convert_fusion
  87.2 31.3 %all_to_all.22 = bf16[32,232,128]{2,1,0:T(8,128)(2,1)S(1)} all-to-all(bf16[32,232,128]{2,1,0:T(8,128)(2,1)S(1)} %add_convert_fusion), channel_id=1, replica_groups=mesh['zh'=4,'y'=4,'core'=2,'zl'=2,'x'=4] {'y','zl','x'}, dimensions={0} | all-to-all | bytes 3801088 | tf_op jit(solution)/shard_map/all_to_all | solution.py:314
  118.5 0.3 convert_reduce_fusion
  118.8 11.1 %all_to_all.23 = f32[4,58,128]{2,1,0:T(8,128)S(1)} all-to-all(f32[4,58,128]{2,1,0:T(8,128)S(1)} %reshape.42), channel_id=1, replica_groups=mesh['zh'=4,'y'=4,'core'=2,'zl'=2,'x'=4] {'zh'}, dimensions={0} | all-to-all | bytes 237568 | tf_op jit(solution)/shard_map/all_to_all | solution.py:316
  130.0 0.8 multiply_subtract_fusion
  (29 shorter events, 0.2 us)
Async XLA Ops:
  18.3 32.1 %copy-start.12 = (s32[256]{0:T(256)S(1)}, s32[256]{0:T(256)}, u32[]{:S(2)}) copy-start(s32[256]{0:T(256)} %param.15) | copy-start | bytes 3076
  18.3 32.3 %copy-start.6 = (s32[256]{0:T(256)S(1)}, s32[256]{0:T(256)}, u32[]{:S(2)}) copy-start(s32[256]{0:T(256)} %param.14) | copy-start | bytes 3076
  18.3 32.4 %copy-start.7 = (bf16[13,25,256]{2,0,1:T(8,128)(2,1)S(1)}, bf16[13,25,256]{2,0,1:T(8,128)(2,1)}, u32[]{:S(2)}) copy-start(bf16[13,25,256]{2,0,1:T(8,128)(2,1)} %param.12) | copy-start | bytes 499204
  18.3 32.5 %copy-start.8 = (bf16[2,256,128]{2,1,0:T(8,128)(2,1)S(1)}, bf16[2,256,128]{2,1,0:T(8,128)(2,1)}, u32[]{:S(2)}) copy-start(bf16[2,256,128]{2,1,0:T(8,128)(2,1)} %param.13) | copy-start | bytes 393220
  18.4 32.5 %copy-start.4 = (bf16[24,25,128]{2,0,1:T(8,128)(2,1)S(1)}, bf16[24,25,128]{2,0,1:T(8,128)(2,1)}, u32[]{:S(2)}) copy-start(bf16[24,25,128]{2,0,1:T(8,128)(2,1)} %param.10) | copy-start | bytes 460804
  49.7 12.8 %collective-permute-start = (bf16[32,232,128]{2,1,0:T(8,128)(2,1)S(1)}, bf16[32,232,128]{2,1,0:T(8,128)(2,1)}, u32[]{:S(2)}, u32[]{:S(2)}) collective-permute-start(bf16[32,232,128]{2,1,0:T(8,128)(2,1)S(1)} %all_to_all.21.mine), channel_id=1, source_target_pairs={{0,8},{8,0},{1,9},{9,1},{2,10},{10,2},{3,11},{11,3},{4,12},{12,4},... | collective-permute-start | bytes 5701640 | tf_op jit(solution)/shard_map/ppermute | solution.py:265
  50.8 11.7 %copy-start.5 = (bf16[24,25,128]{2,0,1:T(8,128)(2,1)S(1)}, bf16[24,25,128]{2,0,1:T(8,128)(2,1)}, u32[]{:S(2)}) copy-start(bf16[24,25,128]{2,0,1:T(8,128)(2,1)} %param.11) | copy-start | bytes 460804
  54.8 2.0 %copy-start = (bf16[13,256,600]{2,1,0:T(8,128)(2,1)}, bf16[13,256,600]{2,1,0:T(8,128)(2,1)S(1)}, u32[]{:S(2)}) copy-start(bf16[13,256,600]{2,1,0:T(8,128)(2,1)S(1)} %get-tuple-element.11.b_far) | copy-start | bytes 11980804
  56.8 2.0 %copy-start.1 = (bf16[13,256,600]{2,1,0:T(8,128)(2,1)}, bf16[13,256,600]{2,1,0:T(8,128)(2,1)S(1)}, u32[]{:S(2)}) copy-start(bf16[13,256,600]{2,1,0:T(8,128)(2,1)S(1)} %get-tuple-element.13.d_far) | copy-start | bytes 11980804
  58.8 1.9 %copy-start.2 = (bf16[13,600,256]{2,1,0:T(8,128)(2,1)}, bf16[13,600,256]{2,1,0:T(8,128)(2,1)S(1)}, u32[]{:S(2)}) copy-start(bf16[13,600,256]{2,1,0:T(8,128)(2,1)S(1)} %get-tuple-element.12.bt_far) | copy-start | bytes 11980804
  60.7 1.9 %copy-start.3 = (bf16[13,600,256]{2,1,0:T(8,128)(2,1)}, bf16[13,600,256]{2,1,0:T(8,128)(2,1)S(1)}, u32[]{:S(2)}) copy-start(bf16[13,600,256]{2,1,0:T(8,128)(2,1)S(1)} %get-tuple-element.14.dt_far) | copy-start | bytes 11980804
  82.6 4.1 %collective-permute-start.1 = (bf16[32,232,128]{2,1,0:T(8,128)(2,1)S(1)}, bf16[32,232,128]{2,1,0:T(8,128)(2,1)S(1)}, u32[]{:S(2)}, u32[]{:S(2)}) collective-permute-start(bf16[32,232,128]{2,1,0:T(8,128)(2,1)S(1)} %get-tuple-element.16), channel_id=1, source_target_pairs={{0,8},{8,0},{1,9},{9,1},{2,10},{10,2},{3,11},{11,3},{4,12},{12,4},... | collective-permute-start | bytes 5701640 | tf_op jit(solution)/shard_map/ppermute | solution.py:265
  118.5 11.4 %copy-start.9 = (f32[2,3648]{1,0:T(2,128)S(1)}, f32[2,3648]{1,0:T(2,128)}, u32[]{:S(2)}) copy-start(f32[2,3648]{1,0:T(2,128)} %param.17) | copy-start | bytes 87556
  118.5 11.5 %copy-start.10 = (f32[2,3648]{1,0:T(2,128)S(1)}, f32[2,3648]{1,0:T(2,128)}, u32[]{:S(2)}) copy-start(f32[2,3648]{1,0:T(2,128)} %param.18) | copy-start | bytes 87556
  118.5 11.5 %copy-start.11 = (f32[2,3648]{1,0:T(2,128)S(1)}, f32[2,3648]{1,0:T(2,128)}, u32[]{:S(2)}) copy-start(f32[2,3648]{1,0:T(2,128)} %param.19) | copy-start | bytes 87556

commit v2 on v1

--- a/solution.py
+++ b/solution.py
@@ -16,6 +16,7 @@
 NEAR = ("y", "zl", "x")
 FAR = ("zh",)
 LANES = 128
+PAIRS = 128
 
 
 def mm(a, b):
@@ -115,9 +116,8 @@
 
 
 def unpack(core, mine, other, flat, stage):
-    layers = flat.shape[0]
-    part = stage.shape[1] // (SIZES[0] * layers)
-    pair = 2 * part - 1
+    pair = flat.shape[0] // PAIRS
+    part = (pair + 1) // 2
     where = [list(chunks(c)) for c in range(2)]
     first = lax.broadcasted_iota(jnp.int32, (part, LANES), 0) == 0
     for g in range(mine.shape[0]):
@@ -128,26 +128,24 @@
             for row, odd, sender, zh in where[c]:
                 if sender != g:
                     continue
-                for i in range(layers):
-                    at = (zh * layers + i) * part
-                    block = stage[c, at : at + part]
-                    to = row * pair + odd * (part - 1)
-                    if odd:
-                        block = jnp.where(first, block + flat[i, to : to + part], block)
-                    flat[i, to : to + part] = block
-
-
-def take_weights(flat, layer, weights):
+                block = stage[c, zh * part : (zh + 1) * part]
+                to = row * pair + odd * (part - 1)
+                if odd:
+                    block = jnp.where(first, block + flat[to : to + part], block)
+                flat[to : to + part] = block
+
+
+def take_weights(flat, weights):
     for ref, (first, side, step) in zip(weights, pieces(weights[0].shape[0], weights[1].shape[0])):
         for q in range(step):
-            ref[:, q * LANES : (q + 1) * LANES] = flat[layer, pl.ds(first + q, side, stride=step), :].astype(BF16)
-
-
-def put_grads(a_ref, dy_ref, kz, ko, layer, flat):
+            ref[:, q * LANES : (q + 1) * LANES] = flat[pl.ds(first + q, side, stride=step), :].astype(BF16)
+
+
+def put_grads(a_ref, dy_ref, kz, ko, flat):
     def put(grad, piece):
         first, side, step = piece
         for q in range(step):
-            flat[layer, pl.ds(first + q, side, stride=step), :] = grad[:, q * LANES : (q + 1) * LANES]
+            flat[pl.ds(first + q, side, stride=step), :] = grad[:, q * LANES : (q + 1) * LANES]
 
     p0, pr, pi = pieces(kz, ko)
     put(mm_at(a_ref[:, :kz], dy_ref[:, :kz]), p0)
@@ -160,58 +158,81 @@
 
 
 def pack(core, flat, stage, keep, send):
-    layers = flat.shape[0]
-    part = stage.shape[1] // (SIZES[0] * layers)
-    pair = 2 * part - 1
+    pair = flat.shape[0] // PAIRS
+    part = (pair + 1) // 2
     where = [list(chunks(c)) for c in range(2)]
+    if stage.shape[1] > part * SIZES[0]:
+        stage[...] = jnp.zeros_like(stage)
     for g in range(keep.shape[0]):
         for c in range(2):
             for row, odd, sender, zh in where[c]:
                 if sender != g:
                     continue
-                for i in range(layers):
-                    at = (zh * layers + i) * part
-                    to = row * pair + odd * (part - 1)
-                    stage[c, at : at + part] = flat[i, to : to + part]
+                to = row * pair + odd * (part - 1)
+                stage[c, zh * part : (zh + 1) * part] = flat[to : to + part]
         v0, v1 = stage[0], stage[1]
         keep[g] = jnp.where(core == 0, v0, v1).astype(BF16)
         send[g] = jnp.where(core == 0, v1, v0).astype(BF16)
 
 
-def main_kernel(nat, core_ref, mine, other, a0_ref, x_ref, cot_ref, rad_ref, b_far, bt_far, d_far, dt_far,
-                keep, send, flat, stage, w0, wr, wi, a_ref, m_ref, dy_ref, b_ref, bt_ref, d_ref, dt_ref, sems):
-    moves = [
-        pltpu.make_async_copy(far, near, sems.at[i])
-        for i, (far, near) in enumerate(((dt_far, dt_ref), (b_far, b_ref), (d_far, d_ref), (bt_far, bt_ref)))
-    ]
-    for move in moves:
-        move.start()
-    chan = x_ref.shape[1]
-    rows = b_ref.shape[0]
+def fetch(far, near, sems, i):
+    return pltpu.make_async_copy(far, near, sems.at[i])
+
+
+def first_kernel(nat, core_ref, mine, other, a0_ref, x_ref, dt_far, out_ref, h_ref,
+                 flat, stage, w0, wr, wi, m_ref, dt_ref, sems):
+    move = fetch(dt_far, dt_ref, sems, 0)
+    move.start()
+    unpack(core_ref[0], mine, other, flat, stage)
+    take_weights(flat, (w0, wr, wi))
+    mix(a0_ref, w0, wr, wi, m_ref)
+    move.wait()
+    out = x_ref[...].astype(F32) + back_to_nodes(dt_ref, m_ref, x_ref.shape[1]) / AVG
+    out_ref[...] = out
+    h_ref[...] = gate(out, nat).astype(BF16)
+
+
+def second_kernel(nat, core_ref, mine, other, h_ref, cot_ref, rad_ref, b_far, dt_far, d_far,
+                  keep, send, dy_ref, dout_ref, w0, wr, wi,
+                  flat, stage, a_ref, m_ref, b_ref, dt_ref, d_ref, sems):
+    chan = h_ref.shape[1]
     kz, ko = w0.shape[0], wr.shape[0]
-    core = core_ref[0]
+    move_b = fetch(b_far, b_ref, sems, 0)
+    move_dt = fetch(dt_far, dt_ref, sems, 1)
+    move_d = fetch(d_far, d_ref, sems, 2)
+    move_b.start()
+    h1 = h_ref[...]
+    unpack(core_ref[0], mine, other, flat, stage)
+    take_weights(flat, (w0, wr, wi))
+    move_b.wait()
+    move_dt.start()
+    rotate(b_ref, h1, rad_ref[...].astype(F32), a_ref)
+    mix(a_ref, w0, wr, wi, m_ref)
+    move_dt.wait()
+    move_d.start()
+    out2 = h1.astype(F32) + back_to_nodes(dt_ref, m_ref, chan) / AVG
+    dout = gate_back(cot_ref[...].astype(F32), out2, nat)
+    dout_ref[...] = dout
+    dagg = (dout / AVG).astype(BF16)
+    move_d.wait()
+    for k in range(d_ref.shape[0]):
+        dy_ref[:, k * chan : (k + 1) * chan] = mm(d_ref[k], dagg).astype(BF16)
+    put_grads(a_ref, dy_ref, kz, ko, flat)
+    pack(core_ref[0], flat, stage, keep, send)
+
+
+def third_kernel(nat, core_ref, dy1_ref, dout_ref, w0, wr, wi, out_ref, a0_ref, rad_ref, bt_far, d_far,
+                 keep, send, flat, stage, m_ref, dy_ref, bt_ref, d_ref, sems):
+    chan = dout_ref.shape[1]
+    kz, ko = w0.shape[0], wr.shape[0]
+    move_bt = fetch(bt_far, bt_ref, sems, 0)
+    move_d = fetch(d_far, d_ref, sems, 1)
+    move_bt.start()
     rad = rad_ref[...].astype(F32)
-    unpack(core, mine, other, flat, stage)
-    take_weights(flat, 0, (w0, wr, wi))
-    mix(a0_ref, w0, wr, wi, m_ref)
-    moves[0].wait()
-    out1 = x_ref[...].astype(F32) + back_to_nodes(dt_ref, m_ref, chan) / AVG
-    h1 = gate(out1, nat).astype(BF16)
-    moves[1].wait()
-    rotate(b_ref, h1, rad, a_ref)
-    take_weights(flat, 1, (w0, wr, wi))
-    mix(a_ref, w0, wr, wi, m_ref)
-    out2 = h1.astype(F32) + back_to_nodes(dt_ref, m_ref, chan) / AVG
-    dout2 = gate_back(cot_ref[...].astype(F32), out2, nat)
-    dagg = (dout2 / AVG).astype(BF16)
-    moves[2].wait()
-    for k in range(rows):
-        dy_ref[:, k * chan : (k + 1) * chan] = mm(d_ref[k], dagg).astype(BF16)
-    put_grads(a_ref, dy_ref, kz, ko, 1, flat)
-    dp = dy_ref[:, kz : kz + ko]
-    dm = dy_ref[:, kz + ko :]
+    dp = dy1_ref[:, kz : kz + ko]
+    dm = dy1_ref[:, kz + ko :]
     parts = (
-        mm_bt(dy_ref[:, :kz], w0[...]),
+        mm_bt(dy1_ref[:, :kz], w0[...]),
         mm_bt(dp, wr[...]) + mm_bt(dm, wi[...]),
         mm_bt(dm, wr[...]) - mm_bt(dp, wi[...]),
     )
@@ -221,13 +242,15 @@
             piece = part[:, q * chan : (q + 1) * chan].astype(BF16).astype(F32)
             m_ref[:, at : at + chan] = (piece * rad).astype(BF16)
             at += chan
-    moves[3].wait()
-    dh1 = (dout2 + back_to_nodes(bt_ref, m_ref, chan)).astype(BF16).astype(F32)
-    dagg1 = (gate_back(dh1, out1, nat) / AVG).astype(BF16)
-    for k in range(rows):
+    move_bt.wait()
+    move_d.start()
+    dh1 = (dout_ref[...] + back_to_nodes(bt_ref, m_ref, chan)).astype(BF16).astype(F32)
+    dagg1 = (gate_back(dh1, out_ref[...], nat) / AVG).astype(BF16)
+    move_d.wait()
+    for k in range(d_ref.shape[0]):
         dy_ref[:, k * chan : (k + 1) * chan] = mm(d_ref[k], dagg1).astype(BF16)
-    put_grads(a0_ref, dy_ref, kz, ko, 0, flat)
-    pack(core, flat, stage, keep, send)
+    put_grads(a0_ref, dy_ref, kz, ko, flat)
+    pack(core_ref[0], flat, stage, keep, send)
 
 
 def sds(shape, dtype):
@@ -279,9 +302,13 @@
 
     half = params.astype(BF16)
     half = jnp.where(odd, jnp.pad(half, ((0, 0), (spare, 0))), jnp.pad(half, ((0, 0), (0, spare))))
-    got = from_everyone(half.reshape(layers * part, LANES), FAR).reshape(far * layers * part, LANES)
-    mine = from_everyone(got, NEAR)
-    other = swap_core(mine)
+    block = -(-far * part // 8) * 8
+    got = from_everyone(half.reshape(layers * part, LANES), FAR).reshape(far, layers, part, LANES)
+    mine, other = [], []
+    for i in range(layers):
+        rows_i = jnp.pad(got[:, i].reshape(far * part, LANES), ((0, block - far * part), (0, 0)))
+        mine.append(from_everyone(rows_i, NEAR))
+        other.append(swap_core(mine[i]))
 
     x = jnp.transpose(node_feats, (1, 0, 2)).reshape(coef * nat, chan)
     cot = jnp.transpose(cotangent, (1, 0, 2)).reshape(coef * nat, chan)
@@ -296,23 +323,57 @@
         (wigner, edge_src.reshape(1, edges), dst.reshape(1, edges), edge_src.reshape(edges, 1), dst.reshape(edges, 1), x, radial[0]),
         vmem=24 << 20,
     )
-    block = far * layers * part
-    flat = [pltpu.VMEM((layers, (kz * kz + 2 * ko * ko) // LANES, LANES), F32), pltpu.VMEM((2, block, LANES), F32)]
-    weights = [pltpu.VMEM((kz, kz), BF16), pltpu.VMEM((ko, ko), BF16), pltpu.VMEM((ko, ko), BF16)]
+    flat = [pltpu.VMEM(((kz * kz + 2 * ko * ko) // LANES, LANES), F32), pltpu.VMEM((2, block, LANES), F32)]
+    sides = [(kz, kz), (ko, ko), (ko, ko)]
+    weights = [pltpu.VMEM(side, BF16) for side in sides]
     space = pltpu.VMEM((edges, rows * chan), BF16)
-    held = [pltpu.VMEM(m.shape, m.dtype) for m in mats]
-    keep, send = call(
-        functools.partial(main_kernel, nat),
-        [sds((near, block, LANES), BF16)] * 2,
-        (core, mine, other, a0, x, cot, radial[1], b, bt, d, dt),
-        [*flat, *weights, space, space, space, *held, pltpu.SemaphoreType.DMA((len(held),))],
+    tall, long = [pltpu.VMEM(m.shape, m.dtype) for m in mats[:2]]
+    halves = [sds((near, block, LANES), BF16)] * 2
+    node32, node16 = sds((wide, chan), F32), sds((wide, chan), BF16)
+
+    def done(n):
+        return pltpu.SemaphoreType.DMA((n,))
+
+    out1, h1 = call(
+        functools.partial(first_kernel, nat),
+        [node32, node16],
+        (core, mine[0], other[0], a0, x, dt),
+        [*flat, *weights, space, long, done(1)],
         scalars=1,
-        far=len(held),
-        vmem=44 << 20,
-    )
-    pair = (keep.astype(F32) + swap_core(send).astype(F32)).astype(BF16)
-    arrived = lax.all_to_all(pair, NEAR, 0, 0, tiled=True)
-    near_sum = arrived.astype(F32).sum(axis=0).reshape(far, layers * part, LANES)
+        far=1,
+        vmem=24 << 20,
+    )
+    keep1, send1, dy1, dout, *w1 = call(
+        functools.partial(second_kernel, nat),
+        [*halves, act, node32, *[sds(side, BF16) for side in sides]],
+        (core, mine[1], other[1], h1, cot, radial[1], b, dt, d),
+        [*flat, space, space, tall, long, tall, done(3)],
+        scalars=1,
+        far=3,
+        vmem=36 << 20,
+    )
+
+    def chip_sum(keep, send):
+        return (keep.astype(F32) + swap_core(send).astype(F32)).astype(BF16)
+
+    def near_sum_of(pair):
+        return lax.all_to_all(pair, NEAR, 0, 0, tiled=True).astype(F32).sum(axis=0)
+
+    pair1 = chip_sum(keep1, send1)
+    sum1 = near_sum_of(pair1)
+    keep0, send0 = call(
+        functools.partial(third_kernel, nat),
+        halves,
+        (core, dy1, dout, *w1, out1, a0, radial[1], bt, d),
+        [*flat, space, space, long, tall, done(2)],
+        scalars=1,
+        far=2,
+        vmem=32 << 20,
+    )
+    pair0 = chip_sum(keep0, send0)
+    sum0 = near_sum_of(pair0)
+    sums = [v[: far * part].reshape(far, part, LANES) for v in (sum0, sum1)]
+    near_sum = jnp.concatenate(sums, axis=1)
     grad = lax.all_to_all(near_sum, FAR, 0, 0, tiled=True).sum(axis=0).reshape(layers, part * LANES)
     grad = jnp.where(odd, grad[:, spare:], grad[:, :shard])
 

time: 131 us -> 151 us (1.15)
  blocking collectives: 90.2 us -> 27.2 us
  waiting for transfers between devices: 3.51 us -> 56.6 us
  starting transfers between devices: 0.6 us -> 27.5 us
  other arithmetic: 2.42 us -> 4.47 us
    all_to_all x0 -> x4, waiting for transfers between devices: none -> 51.9 us  [the longest x2 26 us: near_sum_of(): return lax.all_to_all(pair, NEAR, 0, 0, tiled=True).astype(F32).sum(axis=0)]
    all_to_all x2 -> x1, blocking collectives: 47.8 us -> 16.5 us  [from_everyone(): return lax.all_to_all(spread, axes, 0, 0, tiled=True)]
    all_to_all x1 -> x0, blocking collectives: 31.3 us -> none  [local(): arrived = lax.all_to_all(pair, NEAR, 0, 0, tiled=True)]
    all_to_all x0 -> x4, starting transfers between devices: none -> 26.7 us  [the longest x2 14.3 us: from_everyone(): return lax.all_to_all(spread, axes, 0, 0, tiled=True)]
    convert_element_type x1 -> x2, other arithmetic: 0.49 us -> 2.51 us  [chip_sum(): return (keep.astype(F32) + swap_core(send).astype(F32)).astype(BF16)]
    unnamed x27 -> x23, local copies, waits for them, and re-layouts: 7.9 us -> 5.96 us
    broadcast_in_dim x4, local copies, waits for them, and re-layouts: 0.31 us -> 2.21 us  [from_everyone(): spread = jnp.broadcast_to(x[None], (count_of(axes), *x.shape))]
    pallas_call x2 -> x4, Pallas kernels: 23.9 us -> 22.7 us  [call(): pl.pallas_call(kernel, out_shape=outs, in_specs=specs, out_specs=[pl.Bloc...]
  transfers between devices with their start and end apart: 2 -> 8, of which waited for: 1 -> 6; matrix products, arithmetic and copies ran while one was open for 0% -> 2% of each run, Pallas kernels for 3% -> 5%
where the time goes in v2:
time: 151 us; the launch traced here: 150 us
  waiting for transfers between devices  56.6 us (37%)
  starting transfers between devices  27.5 us (18%)
  blocking collectives  27.2 us (18%)
  Pallas kernels  22.7 us (15%)
  local copies, waits for them, and re-layouts  9.49 us (6%)
  other arithmetic  4.47 us (3%)
  between operations  1.66 us (1%)
    all_to_all x2, waiting for transfers between devices, near_sum_of(): return lax.all_to_all(pair, NEAR, 0, 0, tiled=True).astype(F32).sum(axis=0)  26 us
    all_to_all x2, waiting for transfers between devices, from_everyone(): return lax.all_to_all(spread, axes, 0, 0, tiled=True)  25.8 us
    pallas_call x4, Pallas kernels, call(): pl.pallas_call(kernel, out_shape=outs, in_specs=specs, out_specs=[pl.Bloc...  22.7 us
    all_to_all x1, blocking collectives, from_everyone(): return lax.all_to_all(spread, axes, 0, 0, tiled=True)  16.5 us
    all_to_all x2, starting transfers between devices, from_everyone(): return lax.all_to_all(spread, axes, 0, 0, tiled=True)  14.3 us
    all_to_all x2, starting transfers between devices, near_sum_of(): return lax.all_to_all(pair, NEAR, 0, 0, tiled=True).astype(F32).sum(axis=0)  12.4 us
    all_to_all x1, blocking collectives, local(): lax.all_to_all(near_sum, FAR, 0, 0, tiled=True).sum(axis=0)  10.8 us
    unnamed x23, local copies, waits for them, and re-layouts  5.96 us
  transfers between devices with their start and end apart: 8, of which 6 were waited for; matrix products, arithmetic and copies ran while one was open for 2% of the time, Pallas kernels for 5%

profile of v2, /device:TPU:4, one launch (start us, length us, event | category | flops | bytes accessed | tf_op | source)
XLA Modules:
  0.0 149.6 jit_solution(12928006161791987880)
XLA Ops:
  1.6 16.5 %all_to_all.30 = bf16[4,58,128]{2,1,0:T(8,128)(2,1)S(1)} all-to-all(bf16[4,58,128]{2,1,0:T(8,128)(2,1)S(1)} %broadcast_in_dim.24), channel_id=1, replica_groups=mesh['zh'=4,'y'=4,'core'=2,'zl'=2,'x'=4] {'zh'}, dimensions={0} | all-to-all | bytes 118784 | tf_op jit(solution)/shard_map/all_to_all | solution.py:284
  18.2 1.1 broadcast_in_dim.26
  19.2 8.0 %all-to-all-start.2 = ((bf16[32,120,128]{2,1,0:T(8,128)(2,1)}), bf16[32,120,128]{2,1,0:T(8,128)(2,1)S(1)}, u32[]{:S(2)}, u32[]{:S(2)}) async-start(bf16[32,120,128]{2,1,0:T(8,128)(2,1)} %broadcast_in_dim.26), calls=%async_computation.2 | async-start | bytes 1966080 | tf_op jit(solution)/shard_map/all_to_all | solution.py:284
  27.4 13.5 %all-to-all-done.2.mine = bf16[32,120,128]{2,1,0:T(8,128)(2,1)S(1)} async-done(((bf16[32,120,128]{2,1,0:T(8,128)(2,1)}), bf16[32,120,128]{2,1,0:T(8,128)(2,1)S(1)}, u32[]{:S(2)}, u32[]{:S(2)}) %all-to-all-start.2) | async-done | bytes 983072 | tf_op jit(solution)/shard_map/all_to_all | solution.py:284
  40.9 1.1 broadcast_in_dim.25
  42.0 6.3 %all-to-all-start.1 = ((bf16[32,120,128]{2,1,0:T(8,128)(2,1)}), bf16[32,120,128]{2,1,0:T(8,128)(2,1)S(1)}, u32[]{:S(2)}, u32[]{:S(2)}) async-start(bf16[32,120,128]{2,1,0:T(8,128)(2,1)} %broadcast_in_dim.25), calls=%async_computation.1 | async-start | bytes 1966080 | tf_op jit(solution)/shard_map/all_to_all | solution.py:284
  49.3 1.0 copy.22.wig_ref
  50.3 12.3 %all-to-all-done.1.mine = bf16[32,120,128]{2,1,0:T(8,128)(2,1)S(1)} async-done(((bf16[32,120,128]{2,1,0:T(8,128)(2,1)}), bf16[32,120,128]{2,1,0:T(8,128)(2,1)S(1)}, u32[]{:S(2)}, u32[]{:S(2)}) %all-to-all-start.1) | async-done | bytes 983072 | tf_op jit(solution)/shard_map/all_to_all | solution.py:284
  63.5 0.9 copy-done.1
  64.4 4.0 %shard_map.121 = (bf16[256,1664]{1,0:T(8,128)(2,1)S(1)}, bf16[13,256,600]{2,1,0:T(8,128)(2,1)S(1)}, bf16[13,600,256]{2,1,0:T(8,128)(2,1)S(1)}, bf16[13,256,600]{...) custom-call(bf16[13,25,256]{2,1,0:T(8,128)(2,1)S(1)} %copy.22.wig_ref, s32[1,256]{1,0:T(1,128)S(1)} %bitcast.27, ...), custom_call_target="tpu_custom_call" | custom-call | flops 4294967296 | bytes 1048576 | tf_op jit(solution)/shard_map/pallas_call | solution.py:264
  68.4 1.9 %copy-done.5 = bf16[13,600,256]{2,1,0:T(8,128)(2,1)} copy-done((bf16[13,600,256]{2,1,0:T(8,128)(2,1)}, bf16[13,600,256]{2,1,0:T(8,128)(2,1)S(1)}, u32[]{:S(2)}) %copy-start.5) | copy-done | bytes 3993624
  70.3 3.3 %shard_map.122 = (f32[600,128]{1,0:T(8,128)S(1)}, bf16[600,128]{1,0:T(8,128)(2,1)S(1)}) custom-call(s32[1]{0:T(128)} %bitcast.core_ref, bf16[32,120,128]{2,1,0:T(8,128)(2,1)S(1)} %all-to-all-done.2.mine, bf16[32,120,128]{2,1,0:T(8,128)(2,1)S(1)} %collective-permute-done.1.other, bf16[256,1664]{1,0:T(8,128)(2,1)S(1)} %get-tuple-element.19.a0_ref, ...), custom_call_target="tpu_custom_call" | custom-call | flops 4294967296 | bytes 1048576 | tf_op jit(solution)/shard_map/pallas_call | solution.py:264
  73.7 9.5 %shard_map.123 = (bf16[32,120,128]{2,1,0:T(8,128)(2,1)S(1)}, bf16[32,120,128]{2,1,0:T(8,128)(2,1)S(1)}, bf16[256,1664]{1,0:T(8,128)(2,1)S(1)}, f32[600,128]{1,0:...) custom-call(s32[1]{0:T(128)} %bitcast.core_ref, ...), custom_call_target="tpu_custom_call" | custom-call | flops 4294967296 | bytes 1048576 | tf_op jit(solution)/shard_map/pallas_call | solution.py:264
  83.2 2.1 %copy-done.6 = bf16[13,600,256]{2,1,0:T(8,128)(2,1)S(1)} copy-done((bf16[13,600,256]{2,1,0:T(8,128)(2,1)S(1)}, bf16[13,600,256]{2,1,0:T(8,128)(2,1)}, u32[]{:S(2)}) %copy-start.6) | copy-done | bytes 3993624
  85.3 5.9 %shard_map.124 = (bf16[32,120,128]{2,1,0:T(8,128)(2,1)S(1)}, bf16[32,120,128]{2,1,0:T(8,128)(2,1)S(1)}) custom-call(s32[1]{0:T(128)} %bitcast.core_ref, bf16[256,1664]{1,0:T(8,128)(2,1)S(1)} %get-tuple-element.24.dy1_ref, f32[600,128]{1,0:T(8,128)S(1)} %get-tuple-element.25.dout_ref, bf16[640,640]{1,0:T(8,128)(2,1)S(1)} %get-tuple-element.26.w0, ...), custom_call_target="tpu_custom_call" | custom-call | flops 4294967296 | bytes 1048576 | tf_op jit(solution)/shard_map/pallas_call | solution.py:264
  91.7 2.2 %collective-permute-done.2 = bf16[32,120,128]{2,1,0:T(8,128)(2,1)S(1)} collective-permute-done((bf16[32,120,128]{2,1,0:T(8,128)(2,1)S(1)}, bf16[32,120,128]{2,1,0:T(8,128)(2,1)S(1)}, u32[]{:S(2)}, u32[]{:S(2)}) %collective-permute-start.2) | collective-permute-done | bytes 983072 | tf_op jit(solution)/shard_map/ppermute | solution.py:288
  93.9 1.3 add_convert_fusion.1
  95.2 6.3 %all-to-all-start.3 = ((bf16[32,120,128]{2,1,0:T(8,128)(2,1)}), bf16[32,120,128]{2,1,0:T(8,128)(2,1)S(1)}, u32[]{:S(2)}, u32[]{:S(2)}) async-start(bf16[32,120,128]{2,1,0:T(8,128)(2,1)} %add_convert_fusion.1), calls=%async_computation.3 | async-start | bytes 1966080 | tf_op jit(solution)/shard_map/all_to_all | solution.py:360
  101.6 2.6 %collective-permute-done.3 = bf16[32,120,128]{2,1,0:T(8,128)(2,1)S(1)} collective-permute-done((bf16[32,120,128]{2,1,0:T(8,128)(2,1)S(1)}, bf16[32,120,128]{2,1,0:T(8,128)(2,1)S(1)}, u32[]{:S(2)}, u32[]{:S(2)}) %collective-permute-start.3) | collective-permute-done | bytes 983072 | tf_op jit(solution)/shard_map/ppermute | solution.py:288
  104.1 1.2 add_convert_fusion
  105.4 11.7 %all-to-all-done.3 = bf16[32,120,128]{2,1,0:T(8,128)(2,1)S(1)} async-done(((bf16[32,120,128]{2,1,0:T(8,128)(2,1)}), bf16[32,120,128]{2,1,0:T(8,128)(2,1)S(1)}, u32[]{:S(2)}, u32[]{:S(2)}) %all-to-all-start.3) | async-done | bytes 983072 | tf_op jit(solution)/shard_map/all_to_all | solution.py:360
  117.0 6.2 %all-to-all-start.4 = ((bf16[32,120,128]{2,1,0:T(8,128)(2,1)}), bf16[32,120,128]{2,1,0:T(8,128)(2,1)S(1)}, u32[]{:S(2)}, u32[]{:S(2)}) async-start(bf16[32,120,128]{2,1,0:T(8,128)(2,1)} %add_convert_fusion), calls=%async_computation.4 | async-start | bytes 1966080 | tf_op jit(solution)/shard_map/all_to_all | solution.py:360
  123.4 14.4 %all-to-all-done.4 = bf16[32,120,128]{2,1,0:T(8,128)(2,1)S(1)} async-done(((bf16[32,120,128]{2,1,0:T(8,128)(2,1)}), bf16[32,120,128]{2,1,0:T(8,128)(2,1)S(1)}, u32[]{:S(2)}, u32[]{:S(2)}) %all-to-all-start.4) | async-done | bytes 983072 | tf_op jit(solution)/shard_map/all_to_all | solution.py:360
  138.0 10.8 %all_to_all.31 = f32[4,58,128]{2,1,0:T(8,128)S(1)} all-to-all(f32[4,58,128]{2,1,0:T(8,128)S(1)} %pad_maximum_fusion), channel_id=1, replica_groups=mesh['zh'=4,'y'=4,'core'=2,'zl'=2,'x'=4] {'zh'}, dimensions={0} | all-to-all | bytes 237568 | tf_op jit(solution)/shard_map/all_to_all | solution.py:377
  (49 shorter events, 4.1 us)
Async XLA Ops:
  19.2 21.6 %all-to-all-start.2 = ((bf16[32,120,128]{2,1,0:T(8,128)(2,1)}), bf16[32,120,128]{2,1,0:T(8,128)(2,1)S(1)}, u32[]{:S(2)}, u32[]{:S(2)}) async-start(bf16[32,120,128]{2,1,0:T(8,128)(2,1)} %broadcast_in_dim.26), calls=%async_computation.2 | async-start | bytes 1966080 | tf_op jit(solution)/shard_map/all_to_all | solution.py:284
  27.3 21.7 %copy-start.10 = (s32[256]{0:T(256)S(1)}, s32[256]{0:T(256)}, u32[]{:S(2)}) copy-start(s32[256]{0:T(256)} %param.15) | copy-start | bytes 3076
  27.3 21.8 %copy-start = (s32[256]{0:T(256)S(1)}, s32[256]{0:T(256)}, u32[]{:S(2)}) copy-start(s32[256]{0:T(256)} %param.14) | copy-start | bytes 3076
  42.0 20.6 %all-to-all-start.1 = ((bf16[32,120,128]{2,1,0:T(8,128)(2,1)}), bf16[32,120,128]{2,1,0:T(8,128)(2,1)S(1)}, u32[]{:S(2)}, u32[]{:S(2)}) async-start(bf16[32,120,128]{2,1,0:T(8,128)(2,1)} %broadcast_in_dim.25), calls=%async_computation.1 | async-start | bytes 1966080 | tf_op jit(solution)/shard_map/all_to_all | solution.py:284
  48.2 22.0 %collective-permute-start.1 = (bf16[32,120,128]{2,1,0:T(8,128)(2,1)S(1)}, bf16[32,120,128]{2,1,0:T(8,128)(2,1)S(1)}, u32[]{:S(2)}, u32[]{:S(2)}) collective-permute-start(bf16[32,120,128]{2,1,0:T(8,128)(2,1)S(1)} %all-to-all-done.2.mine), channel_id=1, source_target_pairs={{0,8},{8,0},{1,9},{9,1},{2,10},{10,2},{3,11},{11,3},{4,12},{12,4},... | collective-permute-start | bytes 2949128 | tf_op jit(solution)/shard_map/ppermute | solution.py:288
  62.6 11.0 %collective-permute-start = (bf16[32,120,128]{2,1,0:T(8,128)(2,1)S(1)}, bf16[32,120,128]{2,1,0:T(8,128)(2,1)S(1)}, u32[]{:S(2)}, u32[]{:S(2)}) collective-permute-start(bf16[32,120,128]{2,1,0:T(8,128)(2,1)S(1)} %all-to-all-done.1.mine), channel_id=1, source_target_pairs={{0,8},{8,0},{1,9},{9,1},{2,10},{10,2},{3,11},{11,3},{4,12},{12,4},... | collective-permute-start | bytes 2949128 | tf_op jit(solution)/shard_map/ppermute | solution.py:288
  63.5 0.9 copy-start.1
  68.4 1.9 %copy-start.5 = (bf16[13,600,256]{2,1,0:T(8,128)(2,1)}, bf16[13,600,256]{2,1,0:T(8,128)(2,1)S(1)}, u32[]{:S(2)}) copy-start(bf16[13,600,256]{2,1,0:T(8,128)(2,1)S(1)} %get-tuple-element.30.bt_far) | copy-start | bytes 11980804
  70.3 3.4 %copy-start.3 = (bf16[13,256,600]{2,1,0:T(8,128)(2,1)}, bf16[13,256,600]{2,1,0:T(8,128)(2,1)S(1)}, u32[]{:S(2)}) copy-start(bf16[13,256,600]{2,1,0:T(8,128)(2,1)S(1)} %get-tuple-element.23.d_far) | copy-start | bytes 11980804
  70.3 3.4 %copy-start.2 = (bf16[24,25,128]{2,0,1:T(8,128)(2,1)S(1)}, bf16[24,25,128]{2,0,1:T(8,128)(2,1)}, u32[]{:S(2)}) copy-start(bf16[24,25,128]{2,0,1:T(8,128)(2,1)} %param.11) | copy-start | bytes 460804
  73.6 9.5 %copy-start.4 = (bf16[13,256,600]{2,1,0:T(8,128)(2,1)S(1)}, bf16[13,256,600]{2,1,0:T(8,128)(2,1)}, u32[]{:S(2)}) copy-start(bf16[13,256,600]{2,1,0:T(8,128)(2,1)} %copy-done.3) | copy-start | bytes 11980804
  83.2 2.1 %copy-start.6 = (bf16[13,600,256]{2,1,0:T(8,128)(2,1)S(1)}, bf16[13,600,256]{2,1,0:T(8,128)(2,1)}, u32[]{:S(2)}) copy-start(bf16[13,600,256]{2,1,0:T(8,128)(2,1)} %copy-done.5) | copy-start | bytes 11980804
  91.2 2.8 %collective-permute-start.2 = (bf16[32,120,128]{2,1,0:T(8,128)(2,1)S(1)}, bf16[32,120,128]{2,1,0:T(8,128)(2,1)S(1)}, u32[]{:S(2)}, u32[]{:S(2)}) collective-permute-start(bf16[32,120,128]{2,1,0:T(8,128)(2,1)S(1)} %get-tuple-element.32), channel_id=1, source_target_pairs={{0,8},{8,0},{1,9},{9,1},{2,10},{10,2},{3,11},{11,3},{4,12},{12,4},... | collective-permute-start | bytes 2949128 | tf_op jit(solution)/shard_map/ppermute | solution.py:288
  95.2 21.8 %all-to-all-start.3 = ((bf16[32,120,128]{2,1,0:T(8,128)(2,1)}), bf16[32,120,128]{2,1,0:T(8,128)(2,1)S(1)}, u32[]{:S(2)}, u32[]{:S(2)}) async-start(bf16[32,120,128]{2,1,0:T(8,128)(2,1)} %add_convert_fusion.1), calls=%async_computation.3 | async-start | bytes 1966080 | tf_op jit(solution)/shard_map/all_to_all | solution.py:360
  101.5 2.7 %collective-permute-start.3 = (bf16[32,120,128]{2,1,0:T(8,128)(2,1)S(1)}, bf16[32,120,128]{2,1,0:T(8,128)(2,1)S(1)}, u32[]{:S(2)}, u32[]{:S(2)}) collective-permute-start(bf16[32,120,128]{2,1,0:T(8,128)(2,1)S(1)} %get-tuple-element.34), channel_id=1, source_target_pairs={{0,8},{8,0},{1,9},{9,1},{2,10},{10,2},{3,11},{11,3},{4,12},{12,4},... | collective-permute-start | bytes 2949128 | tf_op jit(solution)/shard_map/ppermute | solution.py:288
  117.0 20.8 %all-to-all-start.4 = ((bf16[32,120,128]{2,1,0:T(8,128)(2,1)}), bf16[32,120,128]{2,1,0:T(8,128)(2,1)S(1)}, u32[]{:S(2)}, u32[]{:S(2)}) async-start(bf16[32,120,128]{2,1,0:T(8,128)(2,1)} %add_convert_fusion), calls=%async_computation.4 | async-start | bytes 1966080 | tf_op jit(solution)/shard_map/all_to_all | solution.py:360
  123.2 25.6 %copy-start.7 = (f32[2,3648]{1,0:T(2,128)S(1)}, f32[2,3648]{1,0:T(2,128)}, u32[]{:S(2)}) copy-start(f32[2,3648]{1,0:T(2,128)} %param.17) | copy-start | bytes 87556
  123.2 25.6 %copy-start.8 = (f32[2,3648]{1,0:T(2,128)S(1)}, f32[2,3648]{1,0:T(2,128)}, u32[]{:S(2)}) copy-start(f32[2,3648]{1,0:T(2,128)} %param.18) | copy-start | bytes 87556
  123.2 25.6 %copy-start.9 = (f32[2,3648]{1,0:T(2,128)S(1)}, f32[2,3648]{1,0:T(2,128)}, u32[]{:S(2)}) copy-start(f32[2,3648]{1,0:T(2,128)} %param.19) | copy-start | bytes 87556

commit v3 on v1

--- a/solution.py
+++ b/solution.py
@@ -184,20 +184,21 @@
         pltpu.make_async_copy(far, near, sems.at[i])
         for i, (far, near) in enumerate(((dt_far, dt_ref), (b_far, b_ref), (d_far, d_ref), (bt_far, bt_ref)))
     ]
-    for move in moves:
-        move.start()
+    moves[0].start()
     chan = x_ref.shape[1]
     rows = b_ref.shape[0]
     kz, ko = w0.shape[0], wr.shape[0]
     core = core_ref[0]
     rad = rad_ref[...].astype(F32)
     unpack(core, mine, other, flat, stage)
+    moves[1].start()
     take_weights(flat, 0, (w0, wr, wi))
     mix(a0_ref, w0, wr, wi, m_ref)
     moves[0].wait()
     out1 = x_ref[...].astype(F32) + back_to_nodes(dt_ref, m_ref, chan) / AVG
     h1 = gate(out1, nat).astype(BF16)
     moves[1].wait()
+    moves[2].start()
     rotate(b_ref, h1, rad, a_ref)
     take_weights(flat, 1, (w0, wr, wi))
     mix(a_ref, w0, wr, wi, m_ref)
@@ -205,6 +206,7 @@
     dout2 = gate_back(cot_ref[...].astype(F32), out2, nat)
     dagg = (dout2 / AVG).astype(BF16)
     moves[2].wait()
+    moves[3].start()
     for k in range(rows):
         dy_ref[:, k * chan : (k + 1) * chan] = mm(d_ref[k], dagg).astype(BF16)
     put_grads(a_ref, dy_ref, kz, ko, 1, flat)

time: 131 us -> 131 us (level)
  no operation moved by 1% of the time
where the time goes in v3:
time: 131 us
  blocking collectives  90.2 us (69%)
  Pallas kernels  23.9 us (18%)
  local copies, waits for them, and re-layouts  8.52 us (7%)
  waiting for transfers between devices  3.51 us (3%)
  other arithmetic  2.42 us (2%)
  between operations  1.52 us (1%)
    all_to_all x2, blocking collectives, from_everyone(): return lax.all_to_all(spread, axes, 0, 0, tiled=True)  47.8 us
    all_to_all x1, blocking collectives, local(): arrived = lax.all_to_all(pair, NEAR, 0, 0, tiled=True)  31.3 us
    pallas_call x2, Pallas kernels, call(): pl.pallas_call(kernel, out_shape=outs, in_specs=specs, out_specs=[pl.Bloc...  23.9 us
    all_to_all x1, blocking collectives, local(): lax.all_to_all(near_sum, FAR, 0, 0, tiled=True).sum(axis=0)  11.1 us
    unnamed x27, local copies, waits for them, and re-layouts  7.9 us
    ppermute x2, waiting for transfers between devices, swap_core(): return lax.ppermute(x, 'core', [(0, 1), (1, 0)])  3.51 us
  transfers between devices with their start and end apart: 2, of which 1 were waited for; matrix products, arithmetic and copies ran while one was open for 0% of the time, Pallas kernels for 3%

profile of v3, /device:TPU:4, one launch (start us, length us, event | category | flops | bytes accessed | tf_op | source)
XLA Modules:
  0.0 130.7 jit_solution(17153405983630542275)
XLA Ops:
  0.6 0.8 convert_element_type.19
  1.4 0.1 broadcast_select_fusion
  1.6 16.5 %all_to_all.20 = bf16[4,58,128]{2,1,0:T(8,128)(2,1)S(1)} all-to-all(bf16[4,58,128]{2,1,0:T(8,128)(2,1)S(1)} %broadcast_in_dim.19), channel_id=1, replica_groups=mesh['zh'=4,'y'=4,'core'=2,'zl'=2,'x'=4] {'zh'}, dimensions={0} | all-to-all | bytes 118784 | tf_op jit(solution)/shard_map/all_to_all | solution.py:263
  18.0 0.2 broadcast_in_dim.21
  18.3 0.0 copy-start.12
  18.3 0.0 copy-start.6
  18.4 0.0 copy-start.4
  18.4 31.4 %all_to_all.21.mine = bf16[32,232,128]{2,1,0:T(8,128)(2,1)S(1)} all-to-all(bf16[32,232,128]{2,1,0:T(8,128)(2,1)S(1)} %broadcast_in_dim.21), channel_id=1, replica_groups=mesh['zh'=4,'y'=4,'core'=2,'zl'=2,'x'=4] {'y','zl','x'}, dimensions={0} | all-to-all | bytes 3801088 | tf_op jit(solution)/shard_map/all_to_all | solution.py:263
  50.4 0.1 copy.16.dstc_ref
  50.6 0.1 copy.15.srcc_ref
  50.7 0.1 copy.14.wig_ref
  50.8 3.9 %shard_map.121 = (bf16[256,1664]{1,0:T(8,128)(2,1)S(1)}, bf16[13,256,600]{2,1,0:T(8,128)(2,1)S(1)}, bf16[13,600,256]{2,1,0:T(8,128)(2,1)S(1)}, bf16[13,256,600]{...) custom-call(bf16[13,25,256]{2,1,0:T(8,128)(2,1)S(1)} %copy.14.wig_ref, s32[1,256]{1,0:T(1,128)S(1)} %bitcast.23, ...), custom_call_target="tpu_custom_call" | custom-call | flops 4294967296 | bytes 1048576 | tf_op jit(solution)/shard_map/pallas_call | solution.py:243
  54.8 2.0 %copy-done = bf16[13,256,600]{2,1,0:T(8,128)(2,1)} copy-done((bf16[13,256,600]{2,1,0:T(8,128)(2,1)}, bf16[13,256,600]{2,1,0:T(8,128)(2,1)S(1)}, u32[]{:S(2)}) %copy-start) | copy-done | bytes 3993624
  56.8 2.0 %copy-done.1 = bf16[13,256,600]{2,1,0:T(8,128)(2,1)} copy-done((bf16[13,256,600]{2,1,0:T(8,128)(2,1)}, bf16[13,256,600]{2,1,0:T(8,128)(2,1)S(1)}, u32[]{:S(2)}) %copy-start.1) | copy-done | bytes 3993624
  58.8 1.9 %copy-done.2 = bf16[13,600,256]{2,1,0:T(8,128)(2,1)} copy-done((bf16[13,600,256]{2,1,0:T(8,128)(2,1)}, bf16[13,600,256]{2,1,0:T(8,128)(2,1)S(1)}, u32[]{:S(2)}) %copy-start.2) | copy-done | bytes 3993624
  60.7 1.9 %copy-done.3 = bf16[13,600,256]{2,1,0:T(8,128)(2,1)} copy-done((bf16[13,600,256]{2,1,0:T(8,128)(2,1)}, bf16[13,600,256]{2,1,0:T(8,128)(2,1)S(1)}, u32[]{:S(2)}) %copy-start.3) | copy-done | bytes 3993624
  62.6 20.0 %shard_map.122 = (bf16[32,232,128]{2,1,0:T(8,128)(2,1)S(1)}, bf16[32,232,128]{2,1,0:T(8,128)(2,1)S(1)}) custom-call(s32[1]{0:T(128)} %bitcast.core_ref, bf16[32,232,128]{2,1,0:T(8,128)(2,1)S(1)} %all_to_all.21.mine, bf16[32,232,128]{2,1,0:T(8,128)(2,1)} %collective-permute-done.other, bf16[256,1664]{1,0:T(8,128)(2,1)S(1)} %get-tuple-element.10.a0_ref, ...), custom_call_target="tpu_custom_call" | custom-call | flops 4294967296 | bytes 1048576 | tf_op jit(solution)/shard_map/pallas_call | solution.py:243
  82.6 0.6 collective-permute-start.1
  83.2 3.5 %collective-permute-done.1 = bf16[32,232,128]{2,1,0:T(8,128)(2,1)S(1)} collective-permute-done((bf16[32,232,128]{2,1,0:T(8,128)(2,1)S(1)}, bf16[32,232,128]{2,1,0:T(8,128)(2,1)S(1)}, u32[]{:S(2)}, u32[]{:S(2)}) %collective-permute-start.1) | collective-permute-done | bytes 1900576 | tf_op jit(solution)/shard_map/ppermute | solution.py:267
  86.7 0.5 add_convert_fusion
  87.2 31.3 %all_to_all.22 = bf16[32,232,128]{2,1,0:T(8,128)(2,1)S(1)} all-to-all(bf16[32,232,128]{2,1,0:T(8,128)(2,1)S(1)} %add_convert_fusion), channel_id=1, replica_groups=mesh['zh'=4,'y'=4,'core'=2,'zl'=2,'x'=4] {'y','zl','x'}, dimensions={0} | all-to-all | bytes 3801088 | tf_op jit(solution)/shard_map/all_to_all | solution.py:316
  118.5 0.3 convert_reduce_fusion
  118.8 11.1 %all_to_all.23 = f32[4,58,128]{2,1,0:T(8,128)S(1)} all-to-all(f32[4,58,128]{2,1,0:T(8,128)S(1)} %reshape.42), channel_id=1, replica_groups=mesh['zh'=4,'y'=4,'core'=2,'zl'=2,'x'=4] {'zh'}, dimensions={0} | all-to-all | bytes 237568 | tf_op jit(solution)/shard_map/all_to_all | solution.py:318
  130.0 0.8 multiply_subtract_fusion
  (29 shorter events, 0.2 us)
Async XLA Ops:
  18.3 32.1 %copy-start.12 = (s32[256]{0:T(256)S(1)}, s32[256]{0:T(256)}, u32[]{:S(2)}) copy-start(s32[256]{0:T(256)} %param.15) | copy-start | bytes 3076
  18.3 32.3 %copy-start.6 = (s32[256]{0:T(256)S(1)}, s32[256]{0:T(256)}, u32[]{:S(2)}) copy-start(s32[256]{0:T(256)} %param.14) | copy-start | bytes 3076
  18.3 32.4 %copy-start.7 = (bf16[13,25,256]{2,0,1:T(8,128)(2,1)S(1)}, bf16[13,25,256]{2,0,1:T(8,128)(2,1)}, u32[]{:S(2)}) copy-start(bf16[13,25,256]{2,0,1:T(8,128)(2,1)} %param.12) | copy-start | bytes 499204
  18.3 32.5 %copy-start.8 = (bf16[2,256,128]{2,1,0:T(8,128)(2,1)S(1)}, bf16[2,256,128]{2,1,0:T(8,128)(2,1)}, u32[]{:S(2)}) copy-start(bf16[2,256,128]{2,1,0:T(8,128)(2,1)} %param.13) | copy-start | bytes 393220
  18.4 32.5 %copy-start.4 = (bf16[24,25,128]{2,0,1:T(8,128)(2,1)S(1)}, bf16[24,25,128]{2,0,1:T(8,128)(2,1)}, u32[]{:S(2)}) copy-start(bf16[24,25,128]{2,0,1:T(8,128)(2,1)} %param.10) | copy-start | bytes 460804
  49.7 12.8 %collective-permute-start = (bf16[32,232,128]{2,1,0:T(8,128)(2,1)S(1)}, bf16[32,232,128]{2,1,0:T(8,128)(2,1)}, u32[]{:S(2)}, u32[]{:S(2)}) collective-permute-start(bf16[32,232,128]{2,1,0:T(8,128)(2,1)S(1)} %all_to_all.21.mine), channel_id=1, source_target_pairs={{0,8},{8,0},{1,9},{9,1},{2,10},{10,2},{3,11},{11,3},{4,12},{12,4},... | collective-permute-start | bytes 5701640 | tf_op jit(solution)/shard_map/ppermute | solution.py:267
  50.8 11.7 %copy-start.5 = (bf16[24,25,128]{2,0,1:T(8,128)(2,1)S(1)}, bf16[24,25,128]{2,0,1:T(8,128)(2,1)}, u32[]{:S(2)}) copy-start(bf16[24,25,128]{2,0,1:T(8,128)(2,1)} %param.11) | copy-start | bytes 460804
  54.8 2.0 %copy-start = (bf16[13,256,600]{2,1,0:T(8,128)(2,1)}, bf16[13,256,600]{2,1,0:T(8,128)(2,1)S(1)}, u32[]{:S(2)}) copy-start(bf16[13,256,600]{2,1,0:T(8,128)(2,1)S(1)} %get-tuple-element.11.b_far) | copy-start | bytes 11980804
  56.8 2.0 %copy-start.1 = (bf16[13,256,600]{2,1,0:T(8,128)(2,1)}, bf16[13,256,600]{2,1,0:T(8,128)(2,1)S(1)}, u32[]{:S(2)}) copy-start(bf16[13,256,600]{2,1,0:T(8,128)(2,1)S(1)} %get-tuple-element.13.d_far) | copy-start | bytes 11980804
  58.8 1.9 %copy-start.2 = (bf16[13,600,256]{2,1,0:T(8,128)(2,1)}, bf16[13,600,256]{2,1,0:T(8,128)(2,1)S(1)}, u32[]{:S(2)}) copy-start(bf16[13,600,256]{2,1,0:T(8,128)(2,1)S(1)} %get-tuple-element.12.bt_far) | copy-start | bytes 11980804
  60.7 1.9 %copy-start.3 = (bf16[13,600,256]{2,1,0:T(8,128)(2,1)}, bf16[13,600,256]{2,1,0:T(8,128)(2,1)S(1)}, u32[]{:S(2)}) copy-start(bf16[13,600,256]{2,1,0:T(8,128)(2,1)S(1)} %get-tuple-element.14.dt_far) | copy-start | bytes 11980804
  82.6 4.1 %collective-permute-start.1 = (bf16[32,232,128]{2,1,0:T(8,128)(2,1)S(1)}, bf16[32,232,128]{2,1,0:T(8,128)(2,1)S(1)}, u32[]{:S(2)}, u32[]{:S(2)}) collective-permute-start(bf16[32,232,128]{2,1,0:T(8,128)(2,1)S(1)} %get-tuple-element.16), channel_id=1, source_target_pairs={{0,8},{8,0},{1,9},{9,1},{2,10},{10,2},{3,11},{11,3},{4,12},{12,4},... | collective-permute-start | bytes 5701640 | tf_op jit(solution)/shard_map/ppermute | solution.py:267
  118.5 11.4 %copy-start.9 = (f32[2,3648]{1,0:T(2,128)S(1)}, f32[2,3648]{1,0:T(2,128)}, u32[]{:S(2)}) copy-start(f32[2,3648]{1,0:T(2,128)} %param.17) | copy-start | bytes 87556
  118.5 11.5 %copy-start.10 = (f32[2,3648]{1,0:T(2,128)S(1)}, f32[2,3648]{1,0:T(2,128)}, u32[]{:S(2)}) copy-start(f32[2,3648]{1,0:T(2,128)} %param.18) | copy-start | bytes 87556
  118.5 11.5 %copy-start.11 = (f32[2,3648]{1,0:T(2,128)S(1)}, f32[2,3648]{1,0:T(2,128)}, u32[]{:S(2)}) copy-start(f32[2,3648]{1,0:T(2,128)} %param.19) | copy-start | bytes 87556

commit v4 on v3

--- a/solution.py
+++ b/solution.py
@@ -13,8 +13,8 @@
 AVG = 10
 AXES = ("zh", "y", "core", "zl", "x")
 SIZES = (4, 4, 2, 2, 4)
-NEAR = ("y", "zl", "x")
-FAR = ("zh",)
+NEAR = ("y", "zl")
+FAR = ("zh", "x")
 LANES = 128
 
 
@@ -104,37 +104,22 @@
     return ((0, kz, kz // LANES), (first, ko, ko // LANES), (second, ko, ko // LANES))
 
 
-def chunks(core):
-    zhs, ys, cores, zls, xs = SIZES
-    for y in range(ys):
-        for zl in range(zls):
-            for x in range(xs):
-                for zh in range(zhs):
-                    owner = (((zh * ys + y) * cores + core) * zls + zl) * xs + x
-                    yield owner // 2, owner % 2, (y * zls + zl) * xs + x, zh
-
-
-def unpack(core, mine, other, flat, stage):
-    layers = flat.shape[0]
-    part = stage.shape[1] // (SIZES[0] * layers)
-    pair = 2 * part - 1
-    where = [list(chunks(c)) for c in range(2)]
-    first = lax.broadcasted_iota(jnp.int32, (part, LANES), 0) == 0
+def chunk_at(g, core, zh):
+    y, zl = divmod(g, SIZES[3])
+    return ((zh * SIZES[1] + y) * SIZES[2] + core) * SIZES[3] + zl
+
+
+def unpack(core, mine, other, layer, flat, stage):
+    rows = stage.shape[1]
+    part = rows // SIZES[0]
     for g in range(mine.shape[0]):
-        m = mine[g].astype(F32)
-        o = other[g].astype(F32)
+        m = mine[g, layer * rows : (layer + 1) * rows].astype(F32)
+        o = other[g, layer * rows : (layer + 1) * rows].astype(F32)
         for c in range(2):
             stage[c] = jnp.where(core == c, m, o)
-            for row, odd, sender, zh in where[c]:
-                if sender != g:
-                    continue
-                for i in range(layers):
-                    at = (zh * layers + i) * part
-                    block = stage[c, at : at + part]
-                    to = row * pair + odd * (part - 1)
-                    if odd:
-                        block = jnp.where(first, block + flat[i, to : to + part], block)
-                    flat[i, to : to + part] = block
+            for zh in range(SIZES[0]):
+                at = chunk_at(g, c, zh) * part
+                flat[layer, at : at + part] = stage[c, zh * part : (zh + 1) * part]
 
 
 def take_weights(flat, layer, weights):
@@ -159,23 +144,17 @@
     put(mm_at(ap, dm) - mm_at(am, dp), pi)
 
 
-def pack(core, flat, stage, keep, send):
-    layers = flat.shape[0]
-    part = stage.shape[1] // (SIZES[0] * layers)
-    pair = 2 * part - 1
-    where = [list(chunks(c)) for c in range(2)]
+def pack(core, layer, flat, stage, keep, send):
+    rows = stage.shape[1]
+    part = rows // SIZES[0]
     for g in range(keep.shape[0]):
         for c in range(2):
-            for row, odd, sender, zh in where[c]:
-                if sender != g:
-                    continue
-                for i in range(layers):
-                    at = (zh * layers + i) * part
-                    to = row * pair + odd * (part - 1)
-                    stage[c, at : at + part] = flat[i, to : to + part]
+            for zh in range(SIZES[0]):
+                at = chunk_at(g, c, zh) * part
+                stage[c, zh * part : (zh + 1) * part] = flat[layer, at : at + part]
         v0, v1 = stage[0], stage[1]
-        keep[g] = jnp.where(core == 0, v0, v1).astype(BF16)
-        send[g] = jnp.where(core == 0, v1, v0).astype(BF16)
+        keep[g, layer * rows : (layer + 1) * rows] = jnp.where(core == 0, v0, v1).astype(BF16)
+        send[g, layer * rows : (layer + 1) * rows] = jnp.where(core == 0, v1, v0).astype(BF16)
 
 
 def main_kernel(nat, core_ref, mine, other, a0_ref, x_ref, cot_ref, rad_ref, b_far, bt_far, d_far, dt_far,
@@ -190,7 +169,7 @@
     kz, ko = w0.shape[0], wr.shape[0]
     core = core_ref[0]
     rad = rad_ref[...].astype(F32)
-    unpack(core, mine, other, flat, stage)
+    unpack(core, mine, other, 0, flat, stage)
     moves[1].start()
     take_weights(flat, 0, (w0, wr, wi))
     mix(a0_ref, w0, wr, wi, m_ref)
@@ -200,6 +179,7 @@
     moves[1].wait()
     moves[2].start()
     rotate(b_ref, h1, rad, a_ref)
+    unpack(core, mine, other, 1, flat, stage)
     take_weights(flat, 1, (w0, wr, wi))
     mix(a_ref, w0, wr, wi, m_ref)
     out2 = h1.astype(F32) + back_to_nodes(dt_ref, m_ref, chan) / AVG
@@ -210,6 +190,7 @@
     for k in range(rows):
         dy_ref[:, k * chan : (k + 1) * chan] = mm(d_ref[k], dagg).astype(BF16)
     put_grads(a_ref, dy_ref, kz, ko, 1, flat)
+    pack(core, 1, flat, stage, keep, send)
     dp = dy_ref[:, kz : kz + ko]
     dm = dy_ref[:, kz + ko :]
     parts = (
@@ -229,7 +210,7 @@
     for k in range(rows):
         dy_ref[:, k * chan : (k + 1) * chan] = mm(d_ref[k], dagg1).astype(BF16)
     put_grads(a0_ref, dy_ref, kz, ko, 0, flat)
-    pack(core, flat, stage, keep, send)
+    pack(core, 0, flat, stage, keep, send)
 
 
 def sds(shape, dtype):
@@ -275,13 +256,11 @@
     layers, shard = params.shape
     far, near = count_of(FAR), count_of(NEAR)
     core = lax.axis_index("core").astype(jnp.int32).reshape(1)
-    odd = lax.axis_index("x") % 2 == 1
-    part = (shard + LANES // 2) // LANES
-    spare = part * LANES - shard
-
-    half = params.astype(BF16)
-    half = jnp.where(odd, jnp.pad(half, ((0, 0), (spare, 0))), jnp.pad(half, ((0, 0), (0, spare))))
-    got = from_everyone(half.reshape(layers * part, LANES), FAR).reshape(far * layers * part, LANES)
+    block = far * shard // LANES
+    lines = layers * shard // LANES
+
+    got = from_everyone(params.astype(BF16).reshape(lines, LANES), FAR).reshape(far, layers, shard)
+    got = jnp.moveaxis(got, 1, 0).reshape(layers * block, LANES)
     mine = from_everyone(got, NEAR)
     other = swap_core(mine)
 
@@ -298,14 +277,13 @@
         (wigner, edge_src.reshape(1, edges), dst.reshape(1, edges), edge_src.reshape(edges, 1), dst.reshape(edges, 1), x, radial[0]),
         vmem=24 << 20,
     )
-    block = far * layers * part
     flat = [pltpu.VMEM((layers, (kz * kz + 2 * ko * ko) // LANES, LANES), F32), pltpu.VMEM((2, block, LANES), F32)]
     weights = [pltpu.VMEM((kz, kz), BF16), pltpu.VMEM((ko, ko), BF16), pltpu.VMEM((ko, ko), BF16)]
     space = pltpu.VMEM((edges, rows * chan), BF16)
     held = [pltpu.VMEM(m.shape, m.dtype) for m in mats]
     keep, send = call(
         functools.partial(main_kernel, nat),
-        [sds((near, block, LANES), BF16)] * 2,
+        [sds((near, layers * block, LANES), BF16)] * 2,
         (core, mine, other, a0, x, cot, radial[1], b, bt, d, dt),
         [*flat, *weights, space, space, space, *held, pltpu.SemaphoreType.DMA((len(held),))],
         scalars=1,
@@ -314,9 +292,9 @@
     )
     pair = (keep.astype(F32) + swap_core(send).astype(F32)).astype(BF16)
     arrived = lax.all_to_all(pair, NEAR, 0, 0, tiled=True)
-    near_sum = arrived.astype(F32).sum(axis=0).reshape(far, layers * part, LANES)
-    grad = lax.all_to_all(near_sum, FAR, 0, 0, tiled=True).sum(axis=0).reshape(layers, part * LANES)
-    grad = jnp.where(odd, grad[:, spare:], grad[:, :shard])
+    near_sum = arrived.astype(F32).sum(axis=0).astype(BF16).reshape(layers, far, shard)
+    near_sum = jnp.moveaxis(near_sum, 1, 0).reshape(far, lines, LANES)
+    grad = lax.all_to_all(near_sum, FAR, 0, 0, tiled=True).astype(F32).sum(axis=0).reshape(layers, shard)
 
     new_moment1 = 0.9 * moment1 + 0.1 * grad
     new_moment2 = 0.95 * moment2 + 0.05 * grad * grad

time: 131 us -> 136 us (1.038)
  blocking collectives: 90.2 us -> 94.1 us
    all_to_all x1, blocking collectives: 11.1 us -> 16.4 us  [local(): lax.all_to_all(near_sum, FAR, 0, 0, tiled=True).astype(F32).sum(axis=0)]
    all_to_all x1, blocking collectives: 31.3 us -> 27.9 us  [local(): arrived = lax.all_to_all(pair, NEAR, 0, 0, tiled=True)]
    all_to_all x2, blocking collectives: 47.8 us -> 49.8 us  [from_everyone(): return lax.all_to_all(spread, axes, 0, 0, tiled=True)]
where the time goes in v4:
time: 136 us
  blocking collectives  94.1 us (69%)
  Pallas kernels  23.8 us (18%)
  local copies, waits for them, and re-layouts  9.8 us (7%)
  waiting for transfers between devices  3.46 us (3%)
  other arithmetic  2.4 us (2%)
  between operations  1.54 us (1%)
    all_to_all x2, blocking collectives, from_everyone(): return lax.all_to_all(spread, axes, 0, 0, tiled=True)  49.8 us
    all_to_all x1, blocking collectives, local(): arrived = lax.all_to_all(pair, NEAR, 0, 0, tiled=True)  27.9 us
    pallas_call x2, Pallas kernels, call(): pl.pallas_call(kernel, out_shape=outs, in_specs=specs, out_specs=[pl.Bloc...  23.8 us
    all_to_all x1, blocking collectives, local(): lax.all_to_all(near_sum, FAR, 0, 0, tiled=True).astype(F32).sum(axis=0)  16.4 us
    unnamed x27, local copies, waits for them, and re-layouts  7.9 us
    ppermute x2, waiting for transfers between devices, swap_core(): return lax.ppermute(x, 'core', [(0, 1), (1, 0)])  3.46 us
  transfers between devices with their start and end apart: 2, of which 1 were waited for; matrix products, arithmetic and copies ran while one was open for 0% of the time, Pallas kernels for 3%

profile of v4, /device:TPU:4, one launch (start us, length us, event | category | flops | bytes accessed | tf_op | source)
XLA Modules:
  0.0 135.7 jit_solution(6784095442022469076)
XLA Ops:
  0.6 0.8 convert_element_type.17
  1.5 22.2 %all_to_all.20 = bf16[16,57,128]{2,1,0:T(8,128)(2,1)S(1)} all-to-all(bf16[16,57,128]{2,1,0:T(8,128)(2,1)S(1)} %broadcast_in_dim.19), channel_id=1, replica_groups=mesh['zh'=4,'y'=4,'core'=2,'zl'=2,'x'=4] {'zh','x'}, dimensions={0} | all-to-all | bytes 466944 | tf_op jit(solution)/shard_map/all_to_all | solution.py:244
  23.7 0.2 reshape.42
  24.0 0.3 broadcast_in_dim.20
  24.3 0.2 broadcast_in_dim.21
  24.6 27.6 %all_to_all.21.mine = bf16[8,912,128]{2,1,0:T(8,128)(2,1)S(1)} all-to-all(bf16[8,912,128]{2,1,0:T(8,128)(2,1)S(1)} %broadcast_in_dim.21), channel_id=1, replica_groups=mesh['zh'=4,'y'=4,'core'=2,'zl'=2,'x'=4] {'y','zl'}, dimensions={0} | all-to-all | bytes 3735552 | tf_op jit(solution)/shard_map/all_to_all | solution.py:244
  52.9 0.1 copy.20.dstc_ref
  53.0 0.1 copy.19.srcc_ref
  53.3 3.9 %shard_map.121 = (bf16[256,1664]{1,0:T(8,128)(2,1)S(1)}, bf16[13,256,600]{2,1,0:T(8,128)(2,1)S(1)}, bf16[13,600,256]{2,1,0:T(8,128)(2,1)S(1)}, bf16[13,256,600]{...) custom-call(bf16[13,25,256]{2,1,0:T(8,128)(2,1)S(1)} %copy.18.wig_ref, s32[1,256]{1,0:T(1,128)S(1)} %bitcast.25, ...), custom_call_target="tpu_custom_call" | custom-call | flops 4294967296 | bytes 1048576 | tf_op jit(solution)/shard_map/pallas_call | solution.py:224
  57.3 2.0 %copy-done = bf16[13,256,600]{2,1,0:T(8,128)(2,1)} copy-done((bf16[13,256,600]{2,1,0:T(8,128)(2,1)}, bf16[13,256,600]{2,1,0:T(8,128)(2,1)S(1)}, u32[]{:S(2)}) %copy-start) | copy-done | bytes 3993624
  59.2 2.0 %copy-done.1 = bf16[13,256,600]{2,1,0:T(8,128)(2,1)} copy-done((bf16[13,256,600]{2,1,0:T(8,128)(2,1)}, bf16[13,256,600]{2,1,0:T(8,128)(2,1)S(1)}, u32[]{:S(2)}) %copy-start.1) | copy-done | bytes 3993624
  61.2 1.9 %copy-done.2 = bf16[13,600,256]{2,1,0:T(8,128)(2,1)} copy-done((bf16[13,600,256]{2,1,0:T(8,128)(2,1)}, bf16[13,600,256]{2,1,0:T(8,128)(2,1)S(1)}, u32[]{:S(2)}) %copy-start.2) | copy-done | bytes 3993624
  63.1 1.9 %copy-done.3 = bf16[13,600,256]{2,1,0:T(8,128)(2,1)} copy-done((bf16[13,600,256]{2,1,0:T(8,128)(2,1)}, bf16[13,600,256]{2,1,0:T(8,128)(2,1)S(1)}, u32[]{:S(2)}) %copy-start.3) | copy-done | bytes 3993624
  65.1 19.8 %shard_map.122 = (bf16[8,912,128]{2,1,0:T(8,128)(2,1)S(1)}, bf16[8,912,128]{2,1,0:T(8,128)(2,1)S(1)}) custom-call(s32[1]{0:T(128)} %bitcast.core_ref, bf16[8,912,128]{2,1,0:T(8,128)(2,1)S(1)} %all_to_all.21.mine, bf16[8,912,128]{2,1,0:T(8,128)(2,1)} %collective-permute-done.other, bf16[256,1664]{1,0:T(8,128)(2,1)S(1)} %get-tuple-element.10.a0_ref, ...), custom_call_target="tpu_custom_call" | custom-call | flops 4294967296 | bytes 1048576 | tf_op jit(solution)/shard_map/pallas_call | solution.py:224
  84.9 0.6 collective-permute-start.1
  85.5 3.5 %collective-permute-done.1 = bf16[8,912,128]{2,1,0:T(8,128)(2,1)S(1)} collective-permute-done((bf16[8,912,128]{2,1,0:T(8,128)(2,1)S(1)}, bf16[8,912,128]{2,1,0:T(8,128)(2,1)S(1)}, u32[]{:S(2)}, u32[]{:S(2)}) %collective-permute-start.1) | collective-permute-done | bytes 1867808 | tf_op jit(solution)/shard_map/ppermute | solution.py:248
  88.9 0.5 add_convert_fusion
  89.5 27.9 %all_to_all.22 = bf16[8,912,128]{2,1,0:T(8,128)(2,1)S(1)} all-to-all(bf16[8,912,128]{2,1,0:T(8,128)(2,1)S(1)} %add_convert_fusion), channel_id=1, replica_groups=mesh['zh'=4,'y'=4,'core'=2,'zl'=2,'x'=4] {'y','zl'}, dimensions={0} | all-to-all | bytes 3735552 | tf_op jit(solution)/shard_map/all_to_all | solution.py:294
  117.4 0.3 reduce_sum.21
  117.7 0.2 reshape.49
  117.9 0.2 copy.21
  118.1 0.2 reshape.50
  118.3 16.4 %all_to_all.23 = bf16[16,57,128]{2,1,0:T(8,128)(2,1)S(1)} all-to-all(bf16[16,57,128]{2,1,0:T(8,128)(2,1)S(1)} %reshape.50), channel_id=1, replica_groups=mesh['zh'=4,'y'=4,'core'=2,'zl'=2,'x'=4] {'zh','x'}, dimensions={0} | all-to-all | bytes 466944 | tf_op jit(solution)/shard_map/all_to_all | solution.py:297
  134.9 0.7 multiply_subtract_fusion
  (32 shorter events, 0.4 us)
Async XLA Ops:
  24.5 28.3 %copy-start.12 = (s32[256]{0:T(256)S(1)}, s32[256]{0:T(256)}, u32[]{:S(2)}) copy-start(s32[256]{0:T(256)} %param.15) | copy-start | bytes 3076
  24.6 28.5 %copy-start.6 = (s32[256]{0:T(256)S(1)}, s32[256]{0:T(256)}, u32[]{:S(2)}) copy-start(s32[256]{0:T(256)} %param.14) | copy-start | bytes 3076
  24.6 28.6 %copy-start.7 = (bf16[13,25,256]{2,0,1:T(8,128)(2,1)S(1)}, bf16[13,25,256]{2,0,1:T(8,128)(2,1)}, u32[]{:S(2)}) copy-start(bf16[13,25,256]{2,0,1:T(8,128)(2,1)} %param.12) | copy-start | bytes 499204
  24.6 28.7 %copy-start.8 = (bf16[2,256,128]{2,1,0:T(8,128)(2,1)S(1)}, bf16[2,256,128]{2,1,0:T(8,128)(2,1)}, u32[]{:S(2)}) copy-start(bf16[2,256,128]{2,1,0:T(8,128)(2,1)} %param.13) | copy-start | bytes 393220
  24.6 28.7 %copy-start.4 = (bf16[24,25,128]{2,0,1:T(8,128)(2,1)S(1)}, bf16[24,25,128]{2,0,1:T(8,128)(2,1)}, u32[]{:S(2)}) copy-start(bf16[24,25,128]{2,0,1:T(8,128)(2,1)} %param.10) | copy-start | bytes 460804
  52.2 12.8 %collective-permute-start = (bf16[8,912,128]{2,1,0:T(8,128)(2,1)S(1)}, bf16[8,912,128]{2,1,0:T(8,128)(2,1)}, u32[]{:S(2)}, u32[]{:S(2)}) collective-permute-start(bf16[8,912,128]{2,1,0:T(8,128)(2,1)S(1)} %all_to_all.21.mine), channel_id=1, source_target_pairs={{0,8},{8,0},{1,9},{9,1},{2,10},{10,2},{3,11},{11,3},{4,12},{12,4},... | collective-permute-start | bytes 5603336 | tf_op jit(solution)/shard_map/ppermute | solution.py:248
  53.3 11.7 %copy-start.5 = (bf16[24,25,128]{2,0,1:T(8,128)(2,1)S(1)}, bf16[24,25,128]{2,0,1:T(8,128)(2,1)}, u32[]{:S(2)}) copy-start(bf16[24,25,128]{2,0,1:T(8,128)(2,1)} %param.11) | copy-start | bytes 460804
  57.2 2.0 %copy-start = (bf16[13,256,600]{2,1,0:T(8,128)(2,1)}, bf16[13,256,600]{2,1,0:T(8,128)(2,1)S(1)}, u32[]{:S(2)}) copy-start(bf16[13,256,600]{2,1,0:T(8,128)(2,1)S(1)} %get-tuple-element.11.b_far) | copy-start | bytes 11980804
  59.2 2.0 %copy-start.1 = (bf16[13,256,600]{2,1,0:T(8,128)(2,1)}, bf16[13,256,600]{2,1,0:T(8,128)(2,1)S(1)}, u32[]{:S(2)}) copy-start(bf16[13,256,600]{2,1,0:T(8,128)(2,1)S(1)} %get-tuple-element.13.d_far) | copy-start | bytes 11980804
  61.2 1.9 %copy-start.2 = (bf16[13,600,256]{2,1,0:T(8,128)(2,1)}, bf16[13,600,256]{2,1,0:T(8,128)(2,1)S(1)}, u32[]{:S(2)}) copy-start(bf16[13,600,256]{2,1,0:T(8,128)(2,1)S(1)} %get-tuple-element.12.bt_far) | copy-start | bytes 11980804
  63.1 1.9 %copy-start.3 = (bf16[13,600,256]{2,1,0:T(8,128)(2,1)}, bf16[13,600,256]{2,1,0:T(8,128)(2,1)S(1)}, u32[]{:S(2)}) copy-start(bf16[13,600,256]{2,1,0:T(8,128)(2,1)S(1)} %get-tuple-element.14.dt_far) | copy-start | bytes 11980804
  84.9 4.0 %collective-permute-start.1 = (bf16[8,912,128]{2,1,0:T(8,128)(2,1)S(1)}, bf16[8,912,128]{2,1,0:T(8,128)(2,1)S(1)}, u32[]{:S(2)}, u32[]{:S(2)}) collective-permute-start(bf16[8,912,128]{2,1,0:T(8,128)(2,1)S(1)} %get-tuple-element.16), channel_id=1, source_target_pairs={{0,8},{8,0},{1,9},{9,1},{2,10},{10,2},{3,11},{11,3},{4,12},{12,4},... | collective-permute-start | bytes 5603336 | tf_op jit(solution)/shard_map/ppermute | solution.py:248
  117.4 17.6 %copy-start.9 = (f32[2,3648]{1,0:T(2,128)S(1)}, f32[2,3648]{1,0:T(2,128)}, u32[]{:S(2)}) copy-start(f32[2,3648]{1,0:T(2,128)} %param.17) | copy-start | bytes 87556
  117.4 17.6 %copy-start.10 = (f32[2,3648]{1,0:T(2,128)S(1)}, f32[2,3648]{1,0:T(2,128)}, u32[]{:S(2)}) copy-start(f32[2,3648]{1,0:T(2,128)} %param.18) | copy-start | bytes 87556
  117.4 17.6 %copy-start.11 = (f32[2,3648]{1,0:T(2,128)S(1)}, f32[2,3648]{1,0:T(2,128)}, u32[]{:S(2)}) copy-start(f32[2,3648]{1,0:T(2,128)} %param.19) | copy-start | bytes 87556

commit v5 on v3

--- a/solution.py
+++ b/solution.py
@@ -52,8 +52,8 @@
         b = e_wide * pick_src
         b_ref[k] = b
         d_ref[k] = e_wide * pick_dst
-        bt_ref[k] = wide_e * pick_src_t
-        dt_ref[k] = wide_e * pick_dst_t
+        bt_ref[:, k * edges : (k + 1) * edges] = wide_e * pick_src_t
+        dt_ref[:, k * edges : (k + 1) * edges] = wide_e * pick_dst_t
         a_ref[:, k * chan : (k + 1) * chan] = (mm(b, x) * rad).astype(BF16)
 
 
@@ -63,20 +63,24 @@
         a_ref[:, k * chan : (k + 1) * chan] = (mm(b_ref[k], x) * rad).astype(BF16)
 
 
+def by_row(value, first, chan, m_ref):
+    edges = value.shape[0]
+    for q in range(value.shape[1] // chan):
+        m_ref[(first + q) * edges : (first + q + 1) * edges] = value[:, q * chan : (q + 1) * chan].astype(BF16)
+
+
 def mix(a_ref, w0, wr, wi, m_ref):
     kz, ko = w0.shape[0], wr.shape[0]
-    m_ref[:, :kz] = mm(a_ref[:, :kz], w0[...]).astype(BF16)
+    chan = m_ref.shape[1]
+    by_row(mm(a_ref[:, :kz], w0[...]), 0, chan, m_ref)
     ap = a_ref[:, kz : kz + ko]
     am = a_ref[:, kz + ko :]
-    m_ref[:, kz : kz + ko] = (mm(ap, wr[...]) - mm(am, wi[...])).astype(BF16)
-    m_ref[:, kz + ko :] = (mm(ap, wi[...]) + mm(am, wr[...])).astype(BF16)
-
-
-def back_to_nodes(t_ref, m_ref, chan):
-    total = mm(t_ref[0], m_ref[:, :chan])
-    for k in range(1, t_ref.shape[0]):
-        total = total + mm(t_ref[k], m_ref[:, k * chan : (k + 1) * chan])
-    return total
+    by_row(mm(ap, wr[...]) - mm(am, wi[...]), kz // chan, chan, m_ref)
+    by_row(mm(ap, wi[...]) + mm(am, wr[...]), (kz + ko) // chan, chan, m_ref)
+
+
+def back_to_nodes(t_ref, m_ref):
+    return mm(t_ref[...], m_ref[...])
 
 
 def gate(out, nat):
@@ -195,14 +199,14 @@
     take_weights(flat, 0, (w0, wr, wi))
     mix(a0_ref, w0, wr, wi, m_ref)
     moves[0].wait()
-    out1 = x_ref[...].astype(F32) + back_to_nodes(dt_ref, m_ref, chan) / AVG
+    out1 = x_ref[...].astype(F32) + back_to_nodes(dt_ref, m_ref) / AVG
     h1 = gate(out1, nat).astype(BF16)
     moves[1].wait()
     moves[2].start()
     rotate(b_ref, h1, rad, a_ref)
     take_weights(flat, 1, (w0, wr, wi))
     mix(a_ref, w0, wr, wi, m_ref)
-    out2 = h1.astype(F32) + back_to_nodes(dt_ref, m_ref, chan) / AVG
+    out2 = h1.astype(F32) + back_to_nodes(dt_ref, m_ref) / AVG
     dout2 = gate_back(cot_ref[...].astype(F32), out2, nat)
     dagg = (dout2 / AVG).astype(BF16)
     moves[2].wait()
@@ -221,10 +225,10 @@
     for part in parts:
         for q in range(part.shape[1] // chan):
             piece = part[:, q * chan : (q + 1) * chan].astype(BF16).astype(F32)
-            m_ref[:, at : at + chan] = (piece * rad).astype(BF16)
-            at += chan
+            by_row(piece * rad, at, chan, m_ref)
+            at += 1
     moves[3].wait()
-    dh1 = (dout2 + back_to_nodes(bt_ref, m_ref, chan)).astype(BF16).astype(F32)
+    dh1 = (dout2 + back_to_nodes(bt_ref, m_ref)).astype(BF16).astype(F32)
     dagg1 = (gate_back(dh1, out1, nat) / AVG).astype(BF16)
     for k in range(rows):
         dy_ref[:, k * chan : (k + 1) * chan] = mm(d_ref[k], dagg1).astype(BF16)
@@ -290,7 +294,7 @@
     live = jnp.arange(edges, dtype=jnp.int32) < edge_count[0]
     dst = jnp.where(live, edge_dst, -1)
     wide = coef * nat
-    mats = [sds((rows, edges, wide), BF16), sds((rows, wide, edges), BF16)] * 2
+    mats = [sds((rows, edges, wide), BF16), sds((wide, rows * edges), BF16)] * 2
     act = sds((edges, rows * chan), BF16)
     a0, b, bt, d, dt = call(
         functools.partial(prep_kernel, nat),
@@ -307,15 +311,15 @@
         functools.partial(main_kernel, nat),
         [sds((near, block, LANES), BF16)] * 2,
         (core, mine, other, a0, x, cot, radial[1], b, bt, d, dt),
-        [*flat, *weights, space, space, space, *held, pltpu.SemaphoreType.DMA((len(held),))],
+        [*flat, *weights, space, pltpu.VMEM((rows * edges, chan), BF16), space, *held, pltpu.SemaphoreType.DMA((len(held),))],
         scalars=1,
         far=len(held),
         vmem=44 << 20,
     )
     pair = (keep.astype(F32) + swap_core(send).astype(F32)).astype(BF16)
     arrived = lax.all_to_all(pair, NEAR, 0, 0, tiled=True)
-    near_sum = arrived.astype(F32).sum(axis=0).reshape(far, layers * part, LANES)
-    grad = lax.all_to_all(near_sum, FAR, 0, 0, tiled=True).sum(axis=0).reshape(layers, part * LANES)
+    near_sum = arrived.astype(F32).sum(axis=0).astype(BF16).reshape(far, layers * part, LANES)
+    grad = lax.all_to_all(near_sum, FAR, 0, 0, tiled=True).astype(F32).sum(axis=0).reshape(layers, part * LANES)
     grad = jnp.where(odd, grad[:, spare:], grad[:, :shard])
 
     new_moment1 = 0.9 * moment1 + 0.1 * grad

time: 131 us -> 133 us (1.015)
  Pallas kernels: 23.9 us -> 25.4 us
    pallas_call x2, Pallas kernels: 23.9 us -> 25.4 us  [call(): pl.pallas_call(kernel, out_shape=outs, in_specs=specs, out_specs=[pl.Bloc...]
where the time goes in v5:
time: 133 us; the launch traced here: 132 us
  blocking collectives  89.7 us (67%)
  Pallas kernels  25.4 us (19%)
  local copies, waits for them, and re-layouts  8.53 us (6%)
  waiting for transfers between devices  3.51 us (3%)
  other arithmetic  2.42 us (2%)
  between operations  1.53 us (1%)
    all_to_all x2, blocking collectives, from_everyone(): return lax.all_to_all(spread, axes, 0, 0, tiled=True)  47.8 us
    all_to_all x1, blocking collectives, local(): arrived = lax.all_to_all(pair, NEAR, 0, 0, tiled=True)  31.3 us
    pallas_call x2, Pallas kernels, call(): pl.pallas_call(kernel, out_shape=outs, in_specs=specs, out_specs=[pl.Bloc...  25.4 us
    all_to_all x1, blocking collectives, local(): lax.all_to_all(near_sum, FAR, 0, 0, tiled=True).astype(F32).sum(axis=0)  10.6 us
    unnamed x27, local copies, waits for them, and re-layouts  7.9 us
    ppermute x2, waiting for transfers between devices, swap_core(): return lax.ppermute(x, 'core', [(0, 1), (1, 0)])  3.51 us
  transfers between devices with their start and end apart: 2, of which 1 were waited for; matrix products, arithmetic and copies ran while one was open for 0% of the time, Pallas kernels for 3%

profile of v5, /device:TPU:4, one launch (start us, length us, event | category | flops | bytes accessed | tf_op | source)
XLA Modules:
  0.0 131.7 jit_solution(2814077657456718755)
XLA Ops:
  0.6 0.8 convert_element_type.21
  1.4 0.1 broadcast_select_fusion
  1.6 16.5 %all_to_all.20 = bf16[4,58,128]{2,1,0:T(8,128)(2,1)S(1)} all-to-all(bf16[4,58,128]{2,1,0:T(8,128)(2,1)S(1)} %broadcast_in_dim.19), channel_id=1, replica_groups=mesh['zh'=4,'y'=4,'core'=2,'zl'=2,'x'=4] {'zh'}, dimensions={0} | all-to-all | bytes 118784 | tf_op jit(solution)/shard_map/all_to_all | solution.py:267
  18.0 0.2 broadcast_in_dim.21
  18.3 0.0 copy-start.12
  18.3 0.0 copy-start.6
  18.4 0.0 copy-start.4
  18.4 31.4 %all_to_all.21.mine = bf16[32,232,128]{2,1,0:T(8,128)(2,1)S(1)} all-to-all(bf16[32,232,128]{2,1,0:T(8,128)(2,1)S(1)} %broadcast_in_dim.21), channel_id=1, replica_groups=mesh['zh'=4,'y'=4,'core'=2,'zl'=2,'x'=4] {'y','zl','x'}, dimensions={0} | all-to-all | bytes 3801088 | tf_op jit(solution)/shard_map/all_to_all | solution.py:267
  50.4 0.1 copy.16.dstc_ref
  50.6 0.1 copy.15.srcc_ref
  50.7 0.1 copy.14.wig_ref
  50.8 3.9 %shard_map.121 = (bf16[256,1664]{1,0:T(8,128)(2,1)S(1)}, bf16[13,256,600]{2,1,0:T(8,128)(2,1)S(1)}, bf16[600,3328]{1,0:T(8,128)(2,1)S(1)}, bf16[13,256,600]{2,1,0:T(8,128)(2,1)S(1)}, bf16[600,3328]{1,0:T(8,128)(2,1)S(1)}) custom-call(bf16[13,25,256]{2,1,0:T(8,128)(2,1)S(1)} %copy.14.wig_ref, s32[1,256]{1,0:T(1,128)S(1)} %bitcast.23, s32[1,256]{1,0:T(1,128)S(1)} %bitcast.21, ...), custom_call_target="tpu_custom_call" | custom-call | flops 4294967296 | bytes 1048576 | tf_op jit(solution)/shard_map/pallas_call | solution.py:247
  54.8 2.0 %copy-done = bf16[13,256,600]{2,1,0:T(8,128)(2,1)} copy-done((bf16[13,256,600]{2,1,0:T(8,128)(2,1)}, bf16[13,256,600]{2,1,0:T(8,128)(2,1)S(1)}, u32[]{:S(2)}) %copy-start) | copy-done | bytes 3993624
  56.8 2.0 %copy-done.1 = bf16[13,256,600]{2,1,0:T(8,128)(2,1)} copy-done((bf16[13,256,600]{2,1,0:T(8,128)(2,1)}, bf16[13,256,600]{2,1,0:T(8,128)(2,1)S(1)}, u32[]{:S(2)}) %copy-start.1) | copy-done | bytes 3993624
  58.8 1.9 %copy-done.2 = bf16[600,3328]{1,0:T(8,128)(2,1)} copy-done((bf16[600,3328]{1,0:T(8,128)(2,1)}, bf16[600,3328]{1,0:T(8,128)(2,1)S(1)}, u32[]{:S(2)}) %copy-start.2) | copy-done | bytes 3993624
  60.7 1.9 %copy-done.3 = bf16[600,3328]{1,0:T(8,128)(2,1)} copy-done((bf16[600,3328]{1,0:T(8,128)(2,1)}, bf16[600,3328]{1,0:T(8,128)(2,1)S(1)}, u32[]{:S(2)}) %copy-start.3) | copy-done | bytes 3993624
  62.6 21.5 %shard_map.122 = (bf16[32,232,128]{2,1,0:T(8,128)(2,1)S(1)}, bf16[32,232,128]{2,1,0:T(8,128)(2,1)S(1)}) custom-call(s32[1]{0:T(128)} %bitcast.core_ref, bf16[32,232,128]{2,1,0:T(8,128)(2,1)S(1)} %all_to_all.21.mine, bf16[32,232,128]{2,1,0:T(8,128)(2,1)} %collective-permute-done.other, bf16[256,1664]{1,0:T(8,128)(2,1)S(1)} %get-tuple-element.10.a0_ref, ...), custom_call_target="tpu_custom_call" | custom-call | flops 4294967296 | bytes 1048576 | tf_op jit(solution)/shard_map/pallas_call | solution.py:247
  84.1 0.6 collective-permute-start.1
  84.7 3.5 %collective-permute-done.1 = bf16[32,232,128]{2,1,0:T(8,128)(2,1)S(1)} collective-permute-done((bf16[32,232,128]{2,1,0:T(8,128)(2,1)S(1)}, bf16[32,232,128]{2,1,0:T(8,128)(2,1)S(1)}, u32[]{:S(2)}, u32[]{:S(2)}) %collective-permute-start.1) | collective-permute-done | bytes 1900576 | tf_op jit(solution)/shard_map/ppermute | solution.py:271
  88.2 0.5 add_convert_fusion
  88.7 31.3 %all_to_all.22 = bf16[32,232,128]{2,1,0:T(8,128)(2,1)S(1)} all-to-all(bf16[32,232,128]{2,1,0:T(8,128)(2,1)S(1)} %add_convert_fusion), channel_id=1, replica_groups=mesh['zh'=4,'y'=4,'core'=2,'zl'=2,'x'=4] {'y','zl','x'}, dimensions={0} | all-to-all | bytes 3801088 | tf_op jit(solution)/shard_map/all_to_all | solution.py:320
  120.0 0.3 reduce_sum.21
  120.3 10.6 %all_to_all.23 = bf16[4,58,128]{2,1,0:T(8,128)(2,1)S(1)} all-to-all(bf16[4,58,128]{2,1,0:T(8,128)(2,1)S(1)} %reshape.42), channel_id=1, replica_groups=mesh['zh'=4,'y'=4,'core'=2,'zl'=2,'x'=4] {'zh'}, dimensions={0} | all-to-all | bytes 118784 | tf_op jit(solution)/shard_map/all_to_all | solution.py:322
  130.9 0.8 multiply_subtract_fusion
  (29 shorter events, 0.2 us)
Async XLA Ops:
  18.3 32.1 %copy-start.12 = (s32[256]{0:T(256)S(1)}, s32[256]{0:T(256)}, u32[]{:S(2)}) copy-start(s32[256]{0:T(256)} %param.15) | copy-start | bytes 3076
  18.3 32.3 %copy-start.6 = (s32[256]{0:T(256)S(1)}, s32[256]{0:T(256)}, u32[]{:S(2)}) copy-start(s32[256]{0:T(256)} %param.14) | copy-start | bytes 3076
  18.3 32.4 %copy-start.7 = (bf16[13,25,256]{2,0,1:T(8,128)(2,1)S(1)}, bf16[13,25,256]{2,0,1:T(8,128)(2,1)}, u32[]{:S(2)}) copy-start(bf16[13,25,256]{2,0,1:T(8,128)(2,1)} %param.12) | copy-start | bytes 499204
  18.3 32.5 %copy-start.8 = (bf16[2,256,128]{2,1,0:T(8,128)(2,1)S(1)}, bf16[2,256,128]{2,1,0:T(8,128)(2,1)}, u32[]{:S(2)}) copy-start(bf16[2,256,128]{2,1,0:T(8,128)(2,1)} %param.13) | copy-start | bytes 393220
  18.4 32.5 %copy-start.4 = (bf16[24,25,128]{2,0,1:T(8,128)(2,1)S(1)}, bf16[24,25,128]{2,0,1:T(8,128)(2,1)}, u32[]{:S(2)}) copy-start(bf16[24,25,128]{2,0,1:T(8,128)(2,1)} %param.10) | copy-start | bytes 460804
  49.7 12.8 %collective-permute-start = (bf16[32,232,128]{2,1,0:T(8,128)(2,1)S(1)}, bf16[32,232,128]{2,1,0:T(8,128)(2,1)}, u32[]{:S(2)}, u32[]{:S(2)}) collective-permute-start(bf16[32,232,128]{2,1,0:T(8,128)(2,1)S(1)} %all_to_all.21.mine), channel_id=1, source_target_pairs={{0,8},{8,0},{1,9},{9,1},{2,10},{10,2},{3,11},{11,3},{4,12},{12,4},... | collective-permute-start | bytes 5701640 | tf_op jit(solution)/shard_map/ppermute | solution.py:271
  50.8 11.7 %copy-start.5 = (bf16[24,25,128]{2,0,1:T(8,128)(2,1)S(1)}, bf16[24,25,128]{2,0,1:T(8,128)(2,1)}, u32[]{:S(2)}) copy-start(bf16[24,25,128]{2,0,1:T(8,128)(2,1)} %param.11) | copy-start | bytes 460804
  54.8 2.0 %copy-start = (bf16[13,256,600]{2,1,0:T(8,128)(2,1)}, bf16[13,256,600]{2,1,0:T(8,128)(2,1)S(1)}, u32[]{:S(2)}) copy-start(bf16[13,256,600]{2,1,0:T(8,128)(2,1)S(1)} %get-tuple-element.11.b_far) | copy-start | bytes 11980804
  56.8 2.0 %copy-start.1 = (bf16[13,256,600]{2,1,0:T(8,128)(2,1)}, bf16[13,256,600]{2,1,0:T(8,128)(2,1)S(1)}, u32[]{:S(2)}) copy-start(bf16[13,256,600]{2,1,0:T(8,128)(2,1)S(1)} %get-tuple-element.13.d_far) | copy-start | bytes 11980804
  58.8 1.9 %copy-start.2 = (bf16[600,3328]{1,0:T(8,128)(2,1)}, bf16[600,3328]{1,0:T(8,128)(2,1)S(1)}, u32[]{:S(2)}) copy-start(bf16[600,3328]{1,0:T(8,128)(2,1)S(1)} %get-tuple-element.12.bt_far) | copy-start | bytes 11980804
  60.7 1.9 %copy-start.3 = (bf16[600,3328]{1,0:T(8,128)(2,1)}, bf16[600,3328]{1,0:T(8,128)(2,1)S(1)}, u32[]{:S(2)}) copy-start(bf16[600,3328]{1,0:T(8,128)(2,1)S(1)} %get-tuple-element.14.dt_far) | copy-start | bytes 11980804
  84.1 4.1 %collective-permute-start.1 = (bf16[32,232,128]{2,1,0:T(8,128)(2,1)S(1)}, bf16[32,232,128]{2,1,0:T(8,128)(2,1)S(1)}, u32[]{:S(2)}, u32[]{:S(2)}) collective-permute-start(bf16[32,232,128]{2,1,0:T(8,128)(2,1)S(1)} %get-tuple-element.16), channel_id=1, source_target_pairs={{0,8},{8,0},{1,9},{9,1},{2,10},{10,2},{3,11},{11,3},{4,12},{12,4},... | collective-permute-start | bytes 5701640 | tf_op jit(solution)/shard_map/ppermute | solution.py:271
  120.0 10.9 %copy-start.9 = (f32[2,3648]{1,0:T(2,128)S(1)}, f32[2,3648]{1,0:T(2,128)}, u32[]{:S(2)}) copy-start(f32[2,3648]{1,0:T(2,128)} %param.17) | copy-start | bytes 87556
  120.0 10.9 %copy-start.10 = (f32[2,3648]{1,0:T(2,128)S(1)}, f32[2,3648]{1,0:T(2,128)}, u32[]{:S(2)}) copy-start(f32[2,3648]{1,0:T(2,128)} %param.18) | copy-start | bytes 87556
  120.0 10.9 %copy-start.11 = (f32[2,3648]{1,0:T(2,128)S(1)}, f32[2,3648]{1,0:T(2,128)}, u32[]{:S(2)}) copy-start(f32[2,3648]{1,0:T(2,128)} %param.19) | copy-start | bytes 87556
